TPU v7x, 32 devices: a whole 2x2x4 slice. The times are simulated.
32 devices in a mesh: gx: 4 (over x, core), gy: 8 (over z, y).
Axes of the slice: x: 2, y: 2, z: 4, core: 2. Of those that a mesh axis runs over, the one named last changes fastest.
Arguments:
- log_crit: float32 [512, 512, 128], P('gx', 'gy'), may hold values from -4 to 4
- col_bins: int32 [512, 512, 4], P('gx', 'gy'), may hold values from 0 to 127
- rate_table: bfloat16 [128, 64], replicated, may hold values from 0.0039978027 to 0.059814453
- tile_mask: int32 [16, 16, 4], P('gx', 'gy'), may hold values from 0 to 1, as said below
- tile_route: int32 [16, 16, 4], P('gx', 'gy'), may hold values from 0 to 7, as said below
- filt_x: float32 [512], replicated, may hold values from 0.1 to 1, as said below
- filt_y: float32 [512], replicated, may hold values from 0.1 to 1, as said below
Outputs:
- recomb: float32 [512, 512, 128], P('gx', 'gy')
- smoothed: float32 [512, 512, 128], P('gx', 'gy')
- load: float32 [4, 8], P('gx', 'gy')
Inputs may be any that keep to these rules, and one draw needn't show every extreme that they name: `tile_mask`: tiles form blocks of 4 x 2 x 4 (indices a // 4, b // 2); among the blocks with the same a // 4, some block has all 32 tiles active. `tile_route`: counting only tiles with tile_mask 1: among the blocks with the same a // 4 at most 16 active tiles share a route, and in every draw some such row of blocks gives every route exactly 16; at most 4 active tiles of one block share a route, and in every draw some block has 4 that do. filt_x[m] == filt_x[512 - m] for 0 < m < 512. filt_y[n] == filt_y[512 - n] for 0 < n < 512.
All inputs are finite; a program needn't handle non-finite values.
Results may differ from a plain program's by a relative error of at most 0.0003.
Values sent between devices are 32-bit elements; how exact they have to be, the bound alone decides.
A program may use at most 128 MiB of HBM per device.

v0:
```python
import functools
import math

import jax
import jax.numpy as jnp
from jax import lax
from jax.experimental import pallas as pl
from jax.experimental.pallas import tpu as pltpu
from jax.sharding import PartitionSpec as P

steepness = 3.0
vmem_grant = 60 * 1024 * 1024
MESH = pl.DeviceIdType.MESH


def node_growth(nodes):
    return [math.exp(steepness * (-2.5 + 5.0 * q / (nodes - 1))) for q in range(nodes // 2, nodes)]


def join(left, right):
    num_left, den_left = left
    num_right, den_right = right
    return (num_left * den_right + num_right * den_left, den_left * den_right)


def integral(field, i, growth, coef_a, coef_b):
    pairs = len(growth)
    v = jnp.exp(field * steepness)
    y = v + jnp.exp(field * -steepness)
    total = None
    for first in range(0, pairs, 4):
        terms = []
        for p in range(first, min(first + 4, pairs)):
            num = coef_a[i, pl.ds(p, 1), :] * v + coef_b[i, pl.ds(p, 1), :]
            terms.append((num, y + (growth[p] + 1.0 / growth[p])))
        while len(terms) > 1:
            terms = [
                join(terms[i], terms[i + 1]) if i + 1 < len(terms) else terms[i]
                for i in range(0, len(terms), 2)
            ]
        part = terms[0][0] * (1.0 / terms[0][1])
        total = part if total is None else total + part
    return total


def eval_kernel(
    growth, tiles, field_ref, bins_ref, live_ref, table_ref, rise_ref, recomb_ref, zfirst_ref,
    sums_ref, turned, values, coef_a, coef_b,
):
    cells_x, rows, depth_all = field_ref.shape
    edge = depth_all // tiles
    pairs = len(growth)
    bins_total = table_ref.shape[1]
    for row in range(rows):
        turned[row] = field_ref[:, row, :].T

    def gather(i, carry):
        levels = lax.broadcasted_iota(jnp.int32, (bins_total, cells_x), 0)
        onehot = jnp.where(levels == bins_ref[pl.ds(i, 1), :], 1.0, 0.0).astype(jnp.bfloat16)
        rows_here = jnp.dot(table_ref[...], onehot, preferred_element_type=jnp.float32)
        rows_here = rows_here * live_ref[pl.ds(i, 1), :]
        upper, lower = rows_here[:pairs], rows_here[pairs:]
        coef_a[i] = upper + lower
        coef_b[i] = upper * rise_ref[1] + lower * rise_ref[0]
        return carry

    def step(i, carry):
        row, tile = i // tiles, i % tiles
        span = pl.ds(pl.multiple_of(tile * edge, edge), edge)
        out = integral(turned[row, span, :], i, growth, coef_a, coef_b)
        values[row, span, :] = out
        sums_ref[pl.ds(i, 1), :] = jnp.sum(out, axis=0, keepdims=True)
        return carry

    lax.fori_loop(0, rows * tiles, gather, 0, unroll=8)
    lax.fori_loop(0, rows * tiles, step, 0)
    for row in range(rows):
        recomb_ref[:, row, :] = values[row].T
        zfirst_ref[:, row, :] = values[row]


def evaluate(log_crit, bins, live, table, growth, tiles):
    cells_x, cells_y, depth_all = log_crit.shape
    rows = 8
    nodes, bins_total = table.shape
    ends = jnp.array([growth, [1.0 / e for e in growth]], jnp.float32)
    rise = jnp.broadcast_to(ends[:, :, None], (2, nodes // 2, cells_x))
    return pl.pallas_call(
        functools.partial(eval_kernel, growth, tiles),
        grid=(cells_y // rows,),
        in_specs=[
            pl.BlockSpec((cells_x, rows, depth_all), lambda j: (0, j, 0)),
            pl.BlockSpec((rows * tiles, cells_x), lambda j: (j, 0)),
            pl.BlockSpec((rows * tiles, cells_x), lambda j: (j, 0)),
            pl.BlockSpec((nodes, bins_total), lambda j: (0, 0)),
            pl.BlockSpec((2, nodes // 2, cells_x), lambda j: (0, 0, 0)),
        ],
        out_specs=[
            pl.BlockSpec((cells_x, rows, depth_all), lambda j: (0, j, 0)),
            pl.BlockSpec((depth_all, rows, cells_x), lambda j: (0, j, 0)),
            pl.BlockSpec((rows * tiles, cells_x), lambda j: (j, 0)),
        ],
        out_shape=[
            jax.ShapeDtypeStruct((cells_x, cells_y, depth_all), jnp.float32),
            jax.ShapeDtypeStruct((depth_all, cells_y, cells_x), jnp.float32),
            jax.ShapeDtypeStruct((cells_y * tiles, cells_x), jnp.float32),
        ],
        scratch_shapes=[
            pltpu.VMEM((rows, depth_all, cells_x), jnp.float32),
            pltpu.VMEM((rows, depth_all, cells_x), jnp.float32),
            pltpu.VMEM((rows * tiles, nodes // 2, cells_x), jnp.float32),
            pltpu.VMEM((rows * tiles, nodes // 2, cells_x), jnp.float32),
        ],
        compiler_params=pltpu.CompilerParams(vmem_limit_bytes=vmem_grant),
        name="evaluate",
    )(log_crit, bins, live, table, rise)


def halves(value):
    high = value.astype(jnp.bfloat16)
    return high, (value - high.astype(jnp.float32)).astype(jnp.bfloat16)


def outer_halves(value):
    high = lax.reduce_precision(value, 8, 7)
    low = lax.reduce_precision(value - high, 8, 7)
    return high.astype(jnp.bfloat16), low.astype(jnp.bfloat16)


def dot3(a_high, a_low, b_high, b_low):
    dot = functools.partial(jnp.dot, preferred_element_type=jnp.float32)
    return dot(a_high, b_high) + (dot(a_high, b_low) + dot(a_low, b_high))


def smooth_kernel(
    span_x, span_y, zfirst, loads, cy_high, cy_low, cx_high, cx_low, out, load_parts,
    plane, done, high, low, send_sem, recv_sem, own_sem, back_send, back_recv, back_own,
    load_sems,
):
    planes, devices, cells_y, cells_x = zfirst.shape
    size_y, size_x = high.shape
    block = 128 if size_y % 128 == 0 else size_y
    gx, gy = lax.axis_index("gx"), lax.axis_index("gy")
    me = gx * span_y + gy

    def at(i, j):
        return {"gx": i, "gy": j}

    def place(ref, k, i, j):
        return ref.at[
            k,
            pl.ds(pl.multiple_of(j * cells_y, cells_y), cells_y),
            pl.ds(pl.multiple_of(i * cells_x, cells_x), cells_x),
        ]

    def each_peer(act):
        def body(n, carry):
            offset_y, offset_x = n // span_x, n % span_x
            act(lax.rem(gx + offset_x, span_x), lax.rem(gy + offset_y, span_y))
            return carry

        lax.fori_loop(1, devices, body, 0)

    barrier = pltpu.get_barrier_semaphore()
    each_peer(
        lambda i, j: pl.semaphore_signal(barrier, inc=1, device_id=at(i, j), device_id_type=MESH)
    )
    for k in range(planes):
        pltpu.make_async_copy(zfirst.at[k, me], place(plane, k, gx, gy), own_sem.at[k]).start()
    pl.semaphore_wait(barrier, devices - 1)

    def send_plane(k):
        def act(i, j):
            pltpu.make_async_remote_copy(
                src_ref=zfirst.at[k, i * span_y + j],
                dst_ref=place(plane, k, gx, gy),
                send_sem=send_sem.at[k],
                recv_sem=recv_sem.at[k],
                device_id=at(i, j),
                device_id_type=MESH,
            ).start()

        each_peer(act)

    def send_back(k):
        def act(i, j):
            pltpu.make_async_remote_copy(
                src_ref=place(done, k, i, j),
                dst_ref=out.at[k, me],
                send_sem=back_send.at[k],
                recv_sem=back_recv.at[k],
                device_id=at(i, j),
                device_id_type=MESH,
            ).start()

        each_peer(act)
        pltpu.make_async_copy(place(done, k, gx, gy), out.at[k, me], back_own.at[k]).start()

    def wait_others(sem, k):
        some = zfirst.at[0, pl.ds(0, devices - 1)]
        pltpu.make_async_copy(some, some, sem.at[k]).wait()

    def wait_own(sem, k):
        one = zfirst.at[0, 0]
        pltpu.make_async_copy(one, one, sem.at[k]).wait()

    own_load = pltpu.make_async_copy(loads.at[gy], load_parts.at[gy], load_sems.at[2])
    own_load.start()

    def send_load(n, carry):
        j = lax.rem(gy + n, span_y)
        pltpu.make_async_remote_copy(
            src_ref=loads.at[j],
            dst_ref=load_parts.at[gy],
            send_sem=load_sems.at[0],
            recv_sem=load_sems.at[1],
            device_id=at(gx, j),
            device_id_type=MESH,
        ).start()
        return carry

    lax.fori_loop(1, span_y, send_load, 0)
    for k in range(planes):
        send_plane(k)

    def finish_plane(k, carry):
        wait_own(own_sem, k)
        wait_others(recv_sem, k)

        def split(r, carry):
            rows = pl.ds(pl.multiple_of(r * block, block), block)
            high[rows, :], low[rows, :] = halves(plane[k, rows, :])
            return carry

        lax.fori_loop(0, size_y // block, split, 0)

        def multiply(r, carry):
            rows = pl.ds(pl.multiple_of(r * block, block), block)
            along_y = dot3(cy_high[rows, :], cy_low[rows, :], high[...], low[...])
            y_high, y_low = halves(along_y)
            done[k, rows, :] = dot3(y_high, y_low, cx_high[...], cx_low[...])
            return carry

        lax.fori_loop(0, size_y // block, multiply, 0)
        send_back(k)
        return carry

    lax.fori_loop(0, planes, finish_plane, 0)
    some_loads = loads.at[pl.ds(0, span_y - 1)]
    pltpu.make_async_copy(some_loads, some_loads, load_sems.at[0]).wait()
    pltpu.make_async_copy(some_loads, some_loads, load_sems.at[1]).wait()
    own_load.wait()
    for k in range(planes):
        wait_others(send_sem, k)
        wait_others(back_send, k)
        wait_own(back_own, k)
        wait_others(back_recv, k)


def smooth(zfirst, loads, cy, cx, span_x, span_y):
    planes, devices, cells_y, cells_x = zfirst.shape
    size_y, size_x = cy.shape[0], cx.shape[0]
    anywhere = pl.BlockSpec(memory_space=pl.ANY)
    inside = pl.BlockSpec(memory_space=pltpu.VMEM)
    sems = pltpu.SemaphoreType.DMA((planes,))
    return pl.pallas_call(
        functools.partial(smooth_kernel, span_x, span_y),
        in_specs=[anywhere] * 2 + [inside] * 4,
        out_specs=[anywhere] * 2,
        out_shape=[
            jax.ShapeDtypeStruct(zfirst.shape, jnp.float32),
            jax.ShapeDtypeStruct(loads.shape, jnp.float32),
        ],
        scratch_shapes=[
            pltpu.VMEM((planes, size_y, size_x), jnp.float32),
            pltpu.VMEM((planes, size_y, size_x), jnp.float32),
            pltpu.VMEM((size_y, size_x), jnp.bfloat16),
            pltpu.VMEM((size_y, size_x), jnp.bfloat16),
        ]
        + [sems] * 6
        + [pltpu.SemaphoreType.DMA((3,))],
        compiler_params=pltpu.CompilerParams(
            collective_id=0, has_side_effects=True, vmem_limit_bytes=vmem_grant
        ),
        name="smooth",
    )(zfirst, loads, *outer_halves(cy), *outer_halves(cx))


def turn_kernel(source_ref, out_ref):
    for row in range(source_ref.shape[1]):
        out_ref[:, row, :] = source_ref[:, row, :].T


def turn(source):
    depth_all, cells_y, cells_x = source.shape
    rows = 8
    return pl.pallas_call(
        turn_kernel,
        grid=(cells_y // rows,),
        in_specs=[pl.BlockSpec((depth_all, rows, cells_x), lambda j: (0, j, 0))],
        out_specs=pl.BlockSpec((cells_x, rows, depth_all), lambda j: (0, j, 0)),
        out_shape=jax.ShapeDtypeStruct((cells_x, cells_y, depth_all), jnp.float32),
        name="turn",
    )(source)


def wave_freq(length):
    half = length // 2
    return jnp.concatenate(
        [jnp.arange(half + 1, dtype=jnp.int32), jnp.arange(1, half, dtype=jnp.int32)]
    )


def wave_table(length):
    half = length // 2
    indices = jnp.arange(length, dtype=jnp.int32)
    turns = indices[:, None] * wave_freq(length)[None, :] % length
    angles = 2.0 * math.pi / length * turns.astype(jnp.float32)
    shift = jnp.where(indices < half + 1, 0.0, math.pi / 2)[None, :]
    return lax.optimization_barrier(jnp.cos(angles - shift))


def circulant(gain, table):
    length = gain.shape[0]
    half = length // 2
    freq = wave_freq(length)
    weight = jnp.concatenate([gain[: half + 1], gain[1:half]])
    doubled = jnp.where((freq == 0) | (freq == half), 1.0, 2.0).astype(jnp.float32)
    scaled = lax.optimization_barrier(table * (weight * doubled / length))
    return lax.dot_general(
        scaled, table, (((1,), (1,)), ((), ())), precision=lax.Precision.HIGHEST
    )


def on_device(log_crit, col_bins, rate_table, tile_mask, tile_route, filt_x, filt_y):
    blocks_x, blocks_y, tiles = tile_mask.shape
    cells_x, cells_y, depth_all = log_crit.shape
    edge = cells_x // blocks_x
    span_x, span_y = lax.axis_size("gx"), lax.axis_size("gy")
    devices = span_x * span_y
    nodes = rate_table.shape[1]
    half = nodes // 2

    bins = col_bins.transpose(1, 2, 0).reshape(cells_y * tiles, cells_x)
    live = (tile_mask == 1).astype(jnp.float32).transpose(1, 2, 0)
    live = jnp.broadcast_to(
        live[:, None, :, :, None], (blocks_y, edge, tiles, blocks_x, edge)
    ).reshape(cells_y * tiles, cells_x)
    table = jnp.concatenate([rate_table[:, half:], rate_table[:, half - 1 :: -1]], axis=1).T

    recomb, zfirst, sums = evaluate(log_crit, bins, live, table, node_growth(nodes), tiles)

    tile_means = jnp.sum(
        sums.reshape(blocks_y, edge, tiles, blocks_x, edge), axis=(1, 4)
    ) / (edge * edge * edge)
    route = tile_route.transpose(1, 2, 0)
    capacity = blocks_x * blocks_y * tiles // 2
    route_ids = jnp.arange(span_y, dtype=jnp.int32)
    contribution = (
        jnp.sum(
            jnp.where(route[..., None] == route_ids, tile_means[..., None], 0.0), axis=(0, 1, 2)
        )
        / capacity
    )
    table_x = wave_table(filt_x.shape[0])
    table_y = table_x if filt_y.shape == filt_x.shape else wave_table(filt_y.shape[0])
    back, load_parts = smooth(
        zfirst.reshape(depth_all // devices, devices, cells_y, cells_x),
        jnp.broadcast_to(contribution[:, None, None], (span_y, 8, 128)),
        circulant(filt_y, table_y), circulant(filt_x, table_x), span_x, span_y,
    )
    device_load = jnp.sum(load_parts[:, 0, 0])
    smoothed = turn(back.reshape(depth_all, cells_y, cells_x))
    return (recomb, smoothed, device_load.reshape(1, 1))


def solution(mesh):
    placed = (
        P("gx", "gy", None),
        P("gx", "gy", None),
        P(),
        P("gx", "gy", None),
        P("gx", "gy", None),
        P(),
        P(),
    )
    return jax.shard_map(
        on_device,
        mesh=mesh,
        in_specs=placed,
        out_specs=(P("gx", "gy", None), P("gx", "gy", None), P("gx", "gy")),
        check_vma=False,
    )
```

profile of v0, /device:TPU:13, one launch (start us, length us, event | category | flops | bytes accessed | tf_op | source)
XLA Modules:
  0.0 272.3 jit_solution(2257193807016664856)
XLA Ops:
  0.6 0.8 slice.26
  1.4 0.8 slice.24
  2.1 0.8 fusion.14
  2.9 0.8 fusion.13
  3.7 0.7 fusion.12
  4.4 0.1 copy.13
  4.5 0.8 copy.14
  5.2 0.7 fusion.16
  6.0 0.6 maximum_bitcast_fusion.table_ref
  6.6 0.1 broadcast_in_dim.54
  6.7 0.9 reshape.105.live_ref
  7.6 3.8 %fusion.8 = f32[512,512]{1,0:T(8,128)S(1)} fusion(f32[512]{0:T(512)S(1)} %get-tuple-element.24, s32[512]{0:T(512)S(1)} %get-tuple-element.15), kind=kLoop, calls=%fused_computation.15 | loop fusion | flops 3932160 | bytes 1052672 | tf_op jit(solution)/shard_map/cos | solution.py:320
  11.4 0.0 copy-start
  11.4 0.3 broadcast_multiply_fusion
  11.7 2.9 %fusion.1 = (bf16[512,512]{1,0:T(8,128)(2,1)}, bf16[512,512]{1,0:T(8,128)(2,1)}) fusion(f32[512,512]{1,0:T(8,128)S(1)} %get-tuple-element.19, f32[512,512]{1,0:T(8,128)S(1)} %fusion.8), kind=kOutput, calls=%fused_computation.8 | convolution fusion | flops 1611923456 | bytes 3145728 | tf_op jit(solution)/shard_map/dot_general | solution.py:330
  14.6 2.9 %fusion.3 = (bf16[512,512]{1,0:T(8,128)(2,1)}, bf16[512,512]{1,0:T(8,128)(2,1)}) fusion(f32[512,512]{1,0:T(8,128)S(1)} %get-tuple-element.18, f32[512,512]{1,0:T(8,128)S(1)} %fusion.8), kind=kOutput, calls=%fused_computation.10 | convolution fusion | flops 1611923456 | bytes 3145728 | tf_op jit(solution)/shard_map/dot_general | solution.py:330
  17.5 0.0 copy-done
  17.5 0.7 broadcast_in_dim.55.rise_ref
  18.1 53.4 %evaluate.1 = (f32[128,64,128]{2,1,0:T(8,128)}, f32[128,64,128]{2,1,0:T(8,128)}, f32[256,128]{1,0:T(8,128)}) custom-call(f32[128,64,128]{2,1,0:T(8,128)} %field_ref.1, s32[256,128]{1,0:T(8,128)} %bitcast.19, f32[256,128]{1,0:T(8,128)} %reshape.105.live_ref, bf16[64,128]{1,0:T(8,128)(2,1)} %maximum_bitcast_fusion.table_ref, ...), custom_call_target="tpu_custom_call" | custom-call | tf_op jit(solution)/shard_map/evaluate/pallas_call | solution.py:88
  71.5 1.2 reshape.107
  72.7 0.2 reduce_sum.27
  72.9 0.1 select_reduce_fusion
  73.0 0.7 broadcast_in_dim.58.loads
  73.7 188.8 %smooth.1 = (f32[4,32,64,128]{3,2,1,0:T(8,128)}, f32[8,8,128]{2,1,0:T(8,128)}) custom-call(f32[4,32,64,128]{3,2,1,0:T(8,128)} %bitcast.17, f32[8,8,128]{2,1,0:T(8,128)} %broadcast_in_dim.58.loads, bf16[512,512]{1,0:T(8,128)(2,1)} %get-tuple-element.21.cy_high, bf16[512,512]{1,0:T(8,128)(2,1)} %get-tuple-element.20.cy_low, ...), custom_call_target="tpu_custom_call" | custom-call | tf_op jit(solution)/shard_map/smooth/pallas_call | solution.py:266
  262.5 1.4 slice_reduce_fusion
  263.9 8.4 %turn.1 = f32[128,64,128]{2,1,0:T(8,128)} custom-call(f32[128,64,128]{2,1,0:T(8,128)} %bitcast.18), custom_call_target="tpu_custom_call" | custom-call | tf_op jit(solution)/shard_map/turn/pallas_call | solution.py:297
  (5 shorter events, 0.0 us)
Async XLA Ops:
  11.4 6.0 %copy-start = (f32[2,32]{1,0:T(2,128)S(1)}, f32[2,32]{1,0:T(2,128)}, u32[]{:S(2)}) copy-start(f32[2,32]{1,0:T(2,128)} %constant.45.clone) | copy-start | bytes 772
where the time goes:
time: 273 us; the launch traced here: 272 us
  Pallas kernels  251 us (92%)
  other arithmetic  8.6 us (3%)
  local copies, waits for them, and re-layouts  6.68 us (2%)
  matrix products  5.73 us (2%)
    pallas_call x1, Pallas kernels, smooth(): pl.pallas_call(functools.partial(smooth_kernel, span_x, span_y), in_specs...  189 us
    pallas_call x1, Pallas kernels, evaluate(): pl.pallas_call(functools.partial(eval_kernel, growth, tiles), grid=(cells...  53.4 us
    pallas_call x1, Pallas kernels, turn(): pl.pallas_call(turn_kernel, grid=(cells_y // rows,), in_specs=[pl.BlockSp...  8.44 us
    dot_general x2, matrix products, circulant(): lax.dot_general(scaled, table, (((1,), (1,)), ((), ())), precision=lax.Pr...  5.73 us

commit v1 on v0

--- a/solution.py
+++ b/solution.py
@@ -11,6 +11,7 @@
 steepness = 3.0
 vmem_grant = 60 * 1024 * 1024
 MESH = pl.DeviceIdType.MESH
+levels = 4
 
 
 def node_growth(nodes):
@@ -132,77 +133,172 @@
     return dot(a_high, b_high) + (dot(a_high, b_low) + dot(a_low, b_high))
 
 
-def smooth_kernel(
-    span_x, span_y, zfirst, loads, cy_high, cy_low, cx_high, cx_low, out, load_parts,
-    plane, done, high, low, send_sem, recv_sem, own_sem, back_send, back_recv, back_own,
-    load_sems,
-):
-    planes, devices, cells_y, cells_x = zfirst.shape
-    size_y, size_x = high.shape
-    block = 128 if size_y % 128 == 0 else size_y
+def share_kernel(span_x, span_y, mine, out, send_sem, recv_sem, own_sem):
+    devices = span_x * span_y
     gx, gy = lax.axis_index("gx"), lax.axis_index("gy")
     me = gx * span_y + gy
 
+    def each_peer(act):
+        def body(n, carry):
+            i = lax.rem(gx + n // span_y, span_x)
+            j = lax.rem(gy + n % span_y, span_y)
+            act({"gx": i, "gy": j})
+            return carry
+
+        lax.fori_loop(1, devices, body, 0)
+
+    barrier = pltpu.get_barrier_semaphore()
+    each_peer(lambda peer: pl.semaphore_signal(barrier, inc=1, device_id=peer, device_id_type=MESH))
+    own = pltpu.make_async_copy(mine, out.at[me], own_sem)
+    own.start()
+    pl.semaphore_wait(barrier, devices - 1)
+
+    def send(peer):
+        pltpu.make_async_remote_copy(
+            src_ref=mine,
+            dst_ref=out.at[me],
+            send_sem=send_sem,
+            recv_sem=recv_sem,
+            device_id=peer,
+            device_id_type=MESH,
+        ).start()
+
+    each_peer(send)
+    own.wait()
+    some = out.at[pl.ds(0, devices - 1)]
+    pltpu.make_async_copy(some, some, send_sem).wait()
+    pltpu.make_async_copy(some, some, recv_sem).wait()
+
+
+def share(mine, span_x, span_y):
+    inside = pl.BlockSpec(memory_space=pltpu.VMEM)
+    return pl.pallas_call(
+        functools.partial(share_kernel, span_x, span_y),
+        in_specs=[inside],
+        out_specs=inside,
+        out_shape=jax.ShapeDtypeStruct((span_x * span_y,) + mine.shape, mine.dtype),
+        scratch_shapes=[pltpu.SemaphoreType.DMA] * 3,
+        compiler_params=pltpu.CompilerParams(collective_id=1, has_side_effects=True),
+        name="share",
+    )(mine)
+
+
+def exchange_kernel(
+    span_x, span_y, edge, zfirst, loads, source_ref, place_ref, cy_high, cy_low, cx_high, cx_low,
+    out, load_parts, own, line, packed, arrived, stage, unpack_stage, high, low,
+    first_send, first_recv, first_own, line_send, line_recv, far_send, far_recv,
+    back_send, back_recv, back_own, load_sems,
+):
+    steps, group, cells_y, cells_x = zfirst.shape
+    size_y, size_x = high.shape
+    part = group // span_x
+    rows = part * cells_y
+    per = 128 // edge
+    packs = packed.shape[1]
+    tiles_x = size_x // edge
+    lane_blocks = size_x // 128
+    tiles = source_ref.shape[1]
+    block = 128
+    gx, gy = lax.axis_index("gx"), lax.axis_index("gy")
+    level, w = gy // part, lax.rem(gy, part)
+    half, side = level // 2, lax.rem(level, 2)
+    mate = 2 * half + 1 - side
+    me = gx * part + w
+    is_middle = (level == 1) | (level == 2)
+    is_end = (level == 0) | (level == 3)
+
     def at(i, j):
         return {"gx": i, "gy": j}
 
-    def place(ref, k, i, j):
+    def place(ref, s, i, j):
         return ref.at[
-            k,
+            s,
             pl.ds(pl.multiple_of(j * cells_y, cells_y), cells_y),
             pl.ds(pl.multiple_of(i * cells_x, cells_x), cells_x),
         ]
 
-    def each_peer(act):
+    def each_of_level(act):
         def body(n, carry):
-            offset_y, offset_x = n // span_x, n % span_x
-            act(lax.rem(gx + offset_x, span_x), lax.rem(gy + offset_y, span_y))
-            return carry
-
-        lax.fori_loop(1, devices, body, 0)
+            act(lax.rem(gx + n // part, span_x), lax.rem(w + n % part, part))
+            return carry
+
+        lax.fori_loop(1, group, body, 0)
+
+    def every_peer(act):
+        def body(n, carry):
+            act(lax.rem(gx + n // span_y, span_x), lax.rem(gy + n % span_y, span_y))
+            return carry
+
+        lax.fori_loop(1, span_x * span_y, body, 0)
 
     barrier = pltpu.get_barrier_semaphore()
-    each_peer(
+    every_peer(
         lambda i, j: pl.semaphore_signal(barrier, inc=1, device_id=at(i, j), device_id_type=MESH)
     )
-    for k in range(planes):
-        pltpu.make_async_copy(zfirst.at[k, me], place(plane, k, gx, gy), own_sem.at[k]).start()
-    pl.semaphore_wait(barrier, devices - 1)
-
-    def send_plane(k):
+    for s in range(steps):
+        pltpu.make_async_copy(zfirst.at[s, me], place(own, s, gx, w), first_own.at[s]).start()
+    pl.semaphore_wait(barrier, span_x * span_y - 1)
+
+    def first(s):
         def act(i, j):
             pltpu.make_async_remote_copy(
-                src_ref=zfirst.at[k, i * span_y + j],
-                dst_ref=place(plane, k, gx, gy),
-                send_sem=send_sem.at[k],
-                recv_sem=recv_sem.at[k],
-                device_id=at(i, j),
+                src_ref=zfirst.at[s, i * part + j],
+                dst_ref=place(own, s, gx, w),
+                send_sem=first_send.at[s],
+                recv_sem=first_recv.at[s],
+                device_id=at(i, level * part + j),
                 device_id_type=MESH,
             ).start()
 
-        each_peer(act)
-
-    def send_back(k):
+        each_of_level(act)
+
+    def send_back(s):
         def act(i, j):
             pltpu.make_async_remote_copy(
-                src_ref=place(done, k, i, j),
-                dst_ref=out.at[k, me],
-                send_sem=back_send.at[k],
-                recv_sem=back_recv.at[k],
-                device_id=at(i, j),
+                src_ref=place(line, s, i, j),
+                dst_ref=out.at[s, me],
+                send_sem=back_send.at[s],
+                recv_sem=back_recv.at[s],
+                device_id=at(i, level * part + j),
                 device_id_type=MESH,
             ).start()
 
-        each_peer(act)
-        pltpu.make_async_copy(place(done, k, gx, gy), out.at[k, me], back_own.at[k]).start()
-
-    def wait_others(sem, k):
-        some = zfirst.at[0, pl.ds(0, devices - 1)]
-        pltpu.make_async_copy(some, some, sem.at[k]).wait()
-
-    def wait_own(sem, k):
+        each_of_level(act)
+        pltpu.make_async_copy(place(line, s, gx, w), out.at[s, me], back_own.at[s]).start()
+
+    def to_mate(source, s):
+        return pltpu.make_async_remote_copy(
+            src_ref=source.at[s],
+            dst_ref=line.at[s],
+            send_sem=line_send.at[s],
+            recv_sem=line_recv.at[s],
+            device_id=at(gx, mate * part + w),
+            device_id_type=MESH,
+        )
+
+    def to_far(s):
+        return pltpu.make_async_remote_copy(
+            src_ref=packed.at[s],
+            dst_ref=arrived.at[s],
+            send_sem=far_send.at[s],
+            recv_sem=far_recv.at[s],
+            device_id=at(gx, (3 - level) * part + w),
+            device_id_type=MESH,
+        )
+
+    def wait_others(sem, s):
+        some = zfirst.at[0, pl.ds(0, group - 1)]
+        pltpu.make_async_copy(some, some, sem.at[s]).wait()
+
+    def wait_own(sem, s):
         one = zfirst.at[0, 0]
-        pltpu.make_async_copy(one, one, sem.at[k]).wait()
+        pltpu.make_async_copy(one, one, sem.at[s]).wait()
+
+    def wait_plane(sem, s):
+        pltpu.make_async_copy(own.at[s], own.at[s], sem.at[s]).wait()
+
+    def wait_packed(sem, s):
+        pltpu.make_async_copy(packed.at[s], packed.at[s], sem.at[s]).wait()
 
     own_load = pltpu.make_async_copy(loads.at[gy], load_parts.at[gy], load_sems.at[2])
     own_load.start()
@@ -220,70 +316,240 @@
         return carry
 
     lax.fori_loop(1, span_y, send_load, 0)
-    for k in range(planes):
-        send_plane(k)
-
-    def finish_plane(k, carry):
-        wait_own(own_sem, k)
-        wait_others(recv_sem, k)
-
-        def split(r, carry):
-            rows = pl.ds(pl.multiple_of(r * block, block), block)
-            high[rows, :], low[rows, :] = halves(plane[k, rows, :])
-            return carry
-
-        lax.fori_loop(0, size_y // block, split, 0)
-
-        def multiply(r, carry):
-            rows = pl.ds(pl.multiple_of(r * block, block), block)
-            along_y = dot3(cy_high[rows, :], cy_low[rows, :], high[...], low[...])
-            y_high, y_low = halves(along_y)
-            done[k, rows, :] = dot3(y_high, y_low, cx_high[...], cx_low[...])
-            return carry
-
-        lax.fori_loop(0, size_y // block, multiply, 0)
-        send_back(k)
+
+    def begin(s, carry):
+        first(s)
         return carry
 
-    lax.fori_loop(0, planes, finish_plane, 0)
+    lax.fori_loop(0, steps, begin, 0)
+
+    lane = lax.broadcasted_iota(jnp.int32, (edge, 128), 1)
+    for r in range(per):
+        unpack_stage[r] = jnp.zeros((edge, 128), jnp.float32)
+
+    def rows_at(start, count):
+        return pl.ds(pl.multiple_of(start, count), count)
+
+    def turns(value):
+        return [value if r == 0 else pltpu.roll(value, r * edge, 1) for r in range(per)]
+
+    def pack(s):
+        def fill(n, carry):
+            down, across = n // lane_blocks, pl.ds(pl.multiple_of(n % lane_blocks * 128, 128), 128)
+            chunk = rows_at(down * edge, edge)
+            strip = rows // edge * lane_blocks
+            for r, value in enumerate(turns(own[s, chunk, across])):
+                stage[(side * strip + n) * per + r] = value
+            for r, value in enumerate(turns(line[s, chunk, across])):
+                stage[((1 - side) * strip + n) * per + r] = value
+            return carry
+
+        lax.fori_loop(0, rows // edge * lane_blocks, fill, 0)
+        t = s // (steps // tiles)
+
+        def one(g, carry):
+            total = None
+            for q in range(per):
+                piece = stage[source_ref[half, t, g * per + q]]
+                total = piece if total is None else jnp.where(lane >= q * edge, piece, total)
+            packed[s, g] = total
+            return carry
+
+        lax.fori_loop(0, packs, one, 0)
+
+    def unpack(s):
+        def fill(g, carry):
+            for r, value in enumerate(turns(arrived[s, g])):
+                unpack_stage[(g + 1) * per + r] = value
+            return carry
+
+        lax.fori_loop(0, packs, fill, 0)
+        t = s // (steps // tiles)
+
+        def one(n, carry):
+            down, block_x = n // lane_blocks, lax.rem(n, lane_blocks)
+            total = None
+            for q in range(per):
+                piece = unpack_stage[place_ref[1 - half, t, n * per + q]]
+                total = piece if total is None else jnp.where(lane >= q * edge, piece, total)
+            to = (
+                rows_at((1 - half) * 2 * rows + down * edge, edge),
+                rows_at(block_x * 128, 128),
+            )
+            high[to], low[to] = halves(total)
+            return carry
+
+        lax.fori_loop(0, 2 * rows // edge * lane_blocks, one, 0)
+
+    def split(source, s, which):
+        def one(r, carry):
+            to = rows_at(which * rows + r * block, block)
+            high[to, :], low[to, :] = halves(source[s, rows_at(r * block, block), :])
+            return carry
+
+        lax.fori_loop(0, rows // block, one, 0)
+
+    def along_y(which, r):
+        chunk = rows_at(which * rows + r * block, block)
+        return dot3(cy_high[chunk, :], cy_low[chunk, :], high[...], low[...])
+
+    def along_x(value):
+        return dot3(*halves(value), cx_high[...], cx_low[...])
+
+    def middle_first(s):
+        wait_own(first_own, s)
+        wait_others(first_recv, s)
+        wait_plane(line_recv, s)
+        pack(s)
+        to_far(s).start()
+
+    def middle_second(s):
+        split(own, s, level)
+        split(line, s, mate)
+        wait_packed(far_recv, s)
+        unpack(s)
+
+        def for_mate(r, carry):
+            own[s, rows_at(r * block, block), :] = along_y(mate, r)
+            return carry
+
+        lax.fori_loop(0, rows // block, for_mate, 0)
+        to_mate(own, s).start()
+
+        def for_me(r, carry):
+            line[s, rows_at(r * block, block), :] = along_x(along_y(level, r))
+            return carry
+
+        lax.fori_loop(0, rows // block, for_me, 0)
+        send_back(s)
+
+    ahead = min(2, steps - 1)
+
+    @pl.when(is_middle)
+    def _():
+        def body(i, carry):
+            @pl.when(i < steps)
+            def _():
+                middle_first(i)
+
+            @pl.when(i >= ahead)
+            def _():
+                middle_second(i - ahead)
+
+            return carry
+
+        lax.fori_loop(0, steps + ahead, body, 0)
+
+        def drain(s, carry):
+            wait_packed(far_send, s)
+            wait_plane(line_send, s)
+            return carry
+
+        lax.fori_loop(0, steps, drain, 0)
+
+    @pl.when(is_end)
+    def _():
+        def feed(s, carry):
+            wait_own(first_own, s)
+            wait_others(first_recv, s)
+            to_mate(own, s).start()
+            return carry
+
+        lax.fori_loop(0, steps, feed, 0)
+
+        def body(s, carry):
+            wait_plane(line_recv, s)
+
+            def for_me(r, carry):
+                line[s, rows_at(r * block, block), :] = along_x(line[s, rows_at(r * block, block), :])
+                return carry
+
+            lax.fori_loop(0, rows // block, for_me, 0)
+            send_back(s)
+            return carry
+
+        lax.fori_loop(0, steps, body, 0)
+
+        def drain(s, carry):
+            wait_plane(line_send, s)
+            return carry
+
+        lax.fori_loop(0, steps, drain, 0)
+
     some_loads = loads.at[pl.ds(0, span_y - 1)]
     pltpu.make_async_copy(some_loads, some_loads, load_sems.at[0]).wait()
     pltpu.make_async_copy(some_loads, some_loads, load_sems.at[1]).wait()
     own_load.wait()
-    for k in range(planes):
-        wait_others(send_sem, k)
-        wait_others(back_send, k)
-        wait_own(back_own, k)
-        wait_others(back_recv, k)
-
-
-def smooth(zfirst, loads, cy, cx, span_x, span_y):
-    planes, devices, cells_y, cells_x = zfirst.shape
-    size_y, size_x = cy.shape[0], cx.shape[0]
+
+    def finish(s, carry):
+        wait_others(first_send, s)
+        wait_others(back_send, s)
+        wait_own(back_own, s)
+        wait_others(back_recv, s)
+        return carry
+
+    lax.fori_loop(0, steps, finish, 0)
+
+
+def exchange(
+    slots, collective, zfirst, loads, source, position, cy_high, cy_low, cx_high, cx_low, span_x,
+    span_y, edge,
+):
+    steps, group, cells_y, cells_x = zfirst.shape
+    size_y, size_x = cy_high.shape[0], cx_high.shape[0]
+    rows = size_y // levels
+    packs = slots * edge // 128
     anywhere = pl.BlockSpec(memory_space=pl.ANY)
     inside = pl.BlockSpec(memory_space=pltpu.VMEM)
-    sems = pltpu.SemaphoreType.DMA((planes,))
+    scalars = pl.BlockSpec(memory_space=pltpu.SMEM)
+    planes = pltpu.VMEM((steps, rows, size_x), jnp.float32)
+    packing = pltpu.VMEM((steps, packs, edge, 128), jnp.float32)
+    sems = pltpu.SemaphoreType.DMA((steps,))
     return pl.pallas_call(
-        functools.partial(smooth_kernel, span_x, span_y),
-        in_specs=[anywhere] * 2 + [inside] * 4,
+        functools.partial(exchange_kernel, span_x, span_y, edge),
+        in_specs=[anywhere] * 2 + [scalars] * 2 + [inside] * 4,
         out_specs=[anywhere] * 2,
         out_shape=[
             jax.ShapeDtypeStruct(zfirst.shape, jnp.float32),
             jax.ShapeDtypeStruct(loads.shape, jnp.float32),
         ],
         scratch_shapes=[
-            pltpu.VMEM((planes, size_y, size_x), jnp.float32),
-            pltpu.VMEM((planes, size_y, size_x), jnp.float32),
+            planes,
+            planes,
+            packing,
+            packing,
+            pltpu.VMEM((2 * rows * size_x // edge // edge, edge, 128), jnp.float32),
+            pltpu.VMEM((128 // edge * (packs + 1), edge, 128), jnp.float32),
             pltpu.VMEM((size_y, size_x), jnp.bfloat16),
             pltpu.VMEM((size_y, size_x), jnp.bfloat16),
         ]
-        + [sems] * 6
+        + [sems] * 10
         + [pltpu.SemaphoreType.DMA((3,))],
         compiler_params=pltpu.CompilerParams(
-            collective_id=0, has_side_effects=True, vmem_limit_bytes=vmem_grant
+            collective_id=collective, has_side_effects=True, vmem_limit_bytes=vmem_grant
         ),
-        name="smooth",
-    )(zfirst, loads, *outer_halves(cy), *outer_halves(cx))
+        name=f"exchange{slots}",
+    )(zfirst, loads, source, position, cy_high, cy_low, cx_high, cx_low)
+
+
+def slot_tables(masks, edge):
+    halves_count = 2
+    flat = masks.reshape(halves_count, -1, masks.shape[2]).transpose(0, 2, 1)
+    slots = flat.shape[2]
+    before = jnp.triu(jnp.ones((slots, slots), jnp.bfloat16), 1)
+    rank = jnp.dot(flat.astype(jnp.bfloat16), before, preferred_element_type=jnp.float32)
+    rank = rank.astype(jnp.int32)
+    per = 128 // edge
+    indices = jnp.arange(slots, dtype=jnp.int32)
+    shifted = (indices % per - rank) % per
+    position = jnp.where(flat == 1, rank, -1)
+    place = jnp.where(flat == 1, (rank // per + 1) * per + shifted, 0)
+    from_place = indices // per * per + (rank - indices) % per
+    source = jnp.sum(
+        jnp.where(position[:, :, None, :] == indices[:, None], from_place[:, :, None, :], 0), axis=3
+    )
+    most = jnp.max(jnp.sum(flat, axis=2))
+    return source, place, most
 
 
 def turn_kernel(source_ref, out_ref):
@@ -364,11 +630,25 @@
     )
     table_x = wave_table(filt_x.shape[0])
     table_y = table_x if filt_y.shape == filt_x.shape else wave_table(filt_y.shape[0])
-    back, load_parts = smooth(
-        zfirst.reshape(depth_all // devices, devices, cells_y, cells_x),
+    mine = jnp.pad((tile_mask == 1).astype(jnp.int32).reshape(1, -1), ((0, 7), (0, 128 - blocks_x * blocks_y * tiles)))
+    masks = share(mine, span_x, span_y)[:, 0, : blocks_x * blocks_y * tiles]
+    masks = masks.reshape(span_x, span_y, blocks_x, blocks_y, tiles).transpose(1, 3, 0, 2, 4)
+    masks = masks.reshape(span_y * blocks_y, span_x * blocks_x, tiles)
+    source, position, most = slot_tables(masks, edge)
+    every = position.shape[2]
+    few = every * 19 // 32
+    group = devices // levels
+    operands = (
+        zfirst.reshape(depth_all // group, group, cells_y, cells_x),
         jnp.broadcast_to(contribution[:, None, None], (span_y, 8, 128)),
-        circulant(filt_y, table_y), circulant(filt_x, table_x), span_x, span_y,
-    )
+        source, position,
+        *outer_halves(circulant(filt_y, table_y)), *outer_halves(circulant(filt_x, table_x)),
+    )
+
+    def run(slots, collective):
+        return lambda *args: exchange(slots, collective, *args, span_x, span_y, edge)
+
+    back, load_parts = lax.cond(most <= few, run(few, 2), run(every, 3), *operands)
     device_load = jnp.sum(load_parts[:, 0, 0])
     smoothed = turn(back.reshape(depth_all, cells_y, cells_x))
     return (recomb, smoothed, device_load.reshape(1, 1))

time: 273 us -> 244 us (0.89)
  the two profiles are of different devices: /device:TPU:13 before, /device:TPU:0 now
where the time goes in v1:
time: 244 us; the launch traced here: 242 us
  Pallas kernels  218 us (89%)
  other arithmetic  11.4 us (5%)
  local copies, waits for them, and re-layouts  7.43 us (3%)
  matrix products  3.89 us (2%)
    pallas_call x1, Pallas kernels, exchange(): pl.pallas_call(functools.partial(exchange_kernel, span_x, span_y, edge),...  144 us
    pallas_call x1, Pallas kernels, evaluate(): pl.pallas_call(functools.partial(eval_kernel, growth, tiles), grid=(cells...  53.3 us
    pallas_call x1, Pallas kernels, share(): pl.pallas_call(functools.partial(share_kernel, span_x, span_y), in_specs=...  12.5 us
    pallas_call x1, Pallas kernels, turn(): pl.pallas_call(turn_kernel, grid=(cells_y // rows,), in_specs=[pl.BlockSp...  8.44 us

profile of v1, /device:TPU:0, one launch (start us, length us, event | category | flops | bytes accessed | tf_op | source)
XLA Modules:
  0.0 242.5 jit_solution(3807159701069741932)
XLA Ops:
  0.7 0.8 slice.36
  1.4 0.8 slice.34
  2.2 0.8 fusion.35
  2.9 0.8 fusion.34
  3.7 0.8 copy.22
  4.5 0.7 convert_bitcast_fusion
  5.2 0.1 copy.18
  5.3 0.1 reshape.158
  5.4 0.6 pad_convert_fusion.mine
  6.0 0.7 fusion.39
  6.7 0.6 maximum_bitcast_fusion.table_ref
  7.3 12.5 %share.1 = s32[32,8,128]{2,1,0:T(8,128)} custom-call(s32[8,128]{1,0:T(8,128)} %pad_convert_fusion.mine), custom_call_target="tpu_custom_call" | custom-call | tf_op jit(solution)/shard_map/share/pallas_call | solution.py:175
  19.8 0.9 slice.32
  20.7 0.1 copy.19
  20.8 0.1 reshape_squeeze.3
  20.9 0.3 copy.20
  21.2 0.2 reshape_reshape.3
  21.3 0.1 bitcast_reduce_fusion
  21.5 0.6 reduce_max.9
  22.8 0.1 negate_select_fusion.4
  22.9 0.1 broadcast_in_dim.121
  23.1 0.9 reshape.157.live_ref
  24.0 3.8 %fusion.22 = f32[512,512]{1,0:T(8,128)S(1)} fusion(f32[512]{0:T(512)S(1)} %get-tuple-element.562, s32[512]{0:T(512)S(1)} %get-tuple-element.540), kind=kLoop, calls=%fused_computation.54 | loop fusion | flops 3932160 | bytes 1052672 | tf_op jit(solution)/shard_map/cos | solution.py:586
  27.8 0.0 copy-start
  27.8 0.3 broadcast_multiply_fusion.4
  28.1 1.9 fusion.15
  30.0 1.9 fusion.17
  31.9 0.0 copy-done
  31.9 0.7 broadcast_in_dim.122.rise_ref
  32.6 53.3 %evaluate.1 = (f32[128,64,128]{2,1,0:T(8,128)}, f32[128,64,128]{2,1,0:T(8,128)}, f32[256,128]{1,0:T(8,128)S(1)}) custom-call(f32[128,64,128]{2,1,0:T(8,128)} %field_ref.1, s32[256,128]{1,0:T(8,128)} %bitcast.44, f32[256,128]{1,0:T(8,128)} %reshape.157.live_ref, bf16[64,128]{1,0:T(8,128)(2,1)} %maximum_bitcast_fusion.table_ref, ...), custom_call_target="tpu_custom_call" | custom-call | tf_op jit(solution)/shard_map/evaluate/pallas_call | solution.py:89
  85.9 148.1 %conditional.1 = (f32[16,8,64,128]{3,2,1,0:T(8,128)}, f32[1,1]{1,0:T(1,128)}) conditional(s32[]{:T(128)} %convert_element_type.26, (f32[128,64,128]{2,1,0:T(8,128)}, s32[2,4,4]{2,1,0:T(4,128)S(1)}, s32[2,4,4,8]{3,2,1,0:T(4,128)S(1)}, f32[256,128]{1,0:T(8,128)S(1)}, pred[2,4,128]{2,1,0:T(4,128)(4,1)S(1)}, /*index=5*/s32[2,4,128]{2,1,0:T(4,128)S(1)}, ...), branch_computations={%region_2.7_spmd, %region_7.12_spmd} | conditional | flops 451335 | bytes 1018680 | solution.py:651
  86.1 0.6 fusion.12
  86.7 0.8 select_reduce_fusion.2.source_ref
  87.5 0.3 reshape.150
  87.8 0.2 reduce_sum.76
  88.0 0.1 select_reduce_fusion.3
  88.1 0.7 broadcast_in_dim.109.loads
  88.8 143.8 %exchange76.2 = (f32[16,8,64,128]{3,2,1,0:T(8,128)}, f32[8,8,128]{2,1,0:T(8,128)}) custom-call(f32[16,8,64,128]{3,2,1,0:T(8,128)} %bitcast.41, f32[8,8,128]{2,1,0:T(8,128)} %broadcast_in_dim.109.loads, s32[2,4,128]{2,1,0:T(4,128)} %select_reduce_fusion.2.source_ref, s32[2,4,128]{2,1,0:T(4,128)} %get-tuple-element.546.place_ref, ...), custom_call_target="tpu_custom_call" | custom-call | tf_op jit(solution)/shard_map/cond/branch_1_fun/exchange76/pallas_call | solution.py:508
  232.6 1.4 slice_reduce_fusion.1
  234.0 8.4 %turn.1 = f32[128,64,128]{2,1,0:T(8,128)} custom-call(f32[128,64,128]{2,1,0:T(8,128)} %bitcast.42), custom_call_target="tpu_custom_call" | custom-call | tf_op jit(solution)/shard_map/turn/pallas_call | solution.py:563
  (18 shorter events, 0.1 us)
Async XLA Ops:
  27.8 4.1 %copy-start = (f32[2,32]{1,0:T(2,128)S(1)}, f32[2,32]{1,0:T(2,128)}, u32[]{:S(2)}) copy-start(f32[2,32]{1,0:T(2,128)} %constant.134.clone) | copy-start | bytes 772

commit v2 on v1

--- a/solution.py
+++ b/solution.py
@@ -3,6 +3,7 @@
 
 import jax
 import jax.numpy as jnp
+import numpy as np
 from jax import lax
 from jax.experimental import pallas as pl
 from jax.experimental.pallas import tpu as pltpu
@@ -24,7 +25,7 @@
     return (num_left * den_right + num_right * den_left, den_left * den_right)
 
 
-def integral(field, i, growth, coef_a, coef_b):
+def integral(field, growth, coef_a, coef_b):
     pairs = len(growth)
     v = jnp.exp(field * steepness)
     y = v + jnp.exp(field * -steepness)
@@ -32,7 +33,7 @@
     for first in range(0, pairs, 4):
         terms = []
         for p in range(first, min(first + 4, pairs)):
-            num = coef_a[i, pl.ds(p, 1), :] * v + coef_b[i, pl.ds(p, 1), :]
+            num = coef_a(p) * v + coef_b(p)
             terms.append((num, y + (growth[p] + 1.0 / growth[p])))
         while len(terms) > 1:
             terms = [
@@ -42,79 +43,6 @@
         part = terms[0][0] * (1.0 / terms[0][1])
         total = part if total is None else total + part
     return total
-
-
-def eval_kernel(
-    growth, tiles, field_ref, bins_ref, live_ref, table_ref, rise_ref, recomb_ref, zfirst_ref,
-    sums_ref, turned, values, coef_a, coef_b,
-):
-    cells_x, rows, depth_all = field_ref.shape
-    edge = depth_all // tiles
-    pairs = len(growth)
-    bins_total = table_ref.shape[1]
-    for row in range(rows):
-        turned[row] = field_ref[:, row, :].T
-
-    def gather(i, carry):
-        levels = lax.broadcasted_iota(jnp.int32, (bins_total, cells_x), 0)
-        onehot = jnp.where(levels == bins_ref[pl.ds(i, 1), :], 1.0, 0.0).astype(jnp.bfloat16)
-        rows_here = jnp.dot(table_ref[...], onehot, preferred_element_type=jnp.float32)
-        rows_here = rows_here * live_ref[pl.ds(i, 1), :]
-        upper, lower = rows_here[:pairs], rows_here[pairs:]
-        coef_a[i] = upper + lower
-        coef_b[i] = upper * rise_ref[1] + lower * rise_ref[0]
-        return carry
-
-    def step(i, carry):
-        row, tile = i // tiles, i % tiles
-        span = pl.ds(pl.multiple_of(tile * edge, edge), edge)
-        out = integral(turned[row, span, :], i, growth, coef_a, coef_b)
-        values[row, span, :] = out
-        sums_ref[pl.ds(i, 1), :] = jnp.sum(out, axis=0, keepdims=True)
-        return carry
-
-    lax.fori_loop(0, rows * tiles, gather, 0, unroll=8)
-    lax.fori_loop(0, rows * tiles, step, 0)
-    for row in range(rows):
-        recomb_ref[:, row, :] = values[row].T
-        zfirst_ref[:, row, :] = values[row]
-
-
-def evaluate(log_crit, bins, live, table, growth, tiles):
-    cells_x, cells_y, depth_all = log_crit.shape
-    rows = 8
-    nodes, bins_total = table.shape
-    ends = jnp.array([growth, [1.0 / e for e in growth]], jnp.float32)
-    rise = jnp.broadcast_to(ends[:, :, None], (2, nodes // 2, cells_x))
-    return pl.pallas_call(
-        functools.partial(eval_kernel, growth, tiles),
-        grid=(cells_y // rows,),
-        in_specs=[
-            pl.BlockSpec((cells_x, rows, depth_all), lambda j: (0, j, 0)),
-            pl.BlockSpec((rows * tiles, cells_x), lambda j: (j, 0)),
-            pl.BlockSpec((rows * tiles, cells_x), lambda j: (j, 0)),
-            pl.BlockSpec((nodes, bins_total), lambda j: (0, 0)),
-            pl.BlockSpec((2, nodes // 2, cells_x), lambda j: (0, 0, 0)),
-        ],
-        out_specs=[
-            pl.BlockSpec((cells_x, rows, depth_all), lambda j: (0, j, 0)),
-            pl.BlockSpec((depth_all, rows, cells_x), lambda j: (0, j, 0)),
-            pl.BlockSpec((rows * tiles, cells_x), lambda j: (j, 0)),
-        ],
-        out_shape=[
-            jax.ShapeDtypeStruct((cells_x, cells_y, depth_all), jnp.float32),
-            jax.ShapeDtypeStruct((depth_all, cells_y, cells_x), jnp.float32),
-            jax.ShapeDtypeStruct((cells_y * tiles, cells_x), jnp.float32),
-        ],
-        scratch_shapes=[
-            pltpu.VMEM((rows, depth_all, cells_x), jnp.float32),
-            pltpu.VMEM((rows, depth_all, cells_x), jnp.float32),
-            pltpu.VMEM((rows * tiles, nodes // 2, cells_x), jnp.float32),
-            pltpu.VMEM((rows * tiles, nodes // 2, cells_x), jnp.float32),
-        ],
-        compiler_params=pltpu.CompilerParams(vmem_limit_bytes=vmem_grant),
-        name="evaluate",
-    )(log_crit, bins, live, table, rise)
 
 
 def halves(value):
@@ -184,20 +112,27 @@
 
 
 def exchange_kernel(
-    span_x, span_y, edge, zfirst, loads, source_ref, place_ref, cy_high, cy_low, cx_high, cx_low,
-    out, load_parts, own, line, packed, arrived, stage, unpack_stage, high, low,
+    span_x, span_y, growth, capacity, log_crit, bins_ref, live_ref, route_ref, table_ref, rise_ref,
+    source_ref, place_ref, cy_high, cy_low, cx_high, cx_low,
+    recomb, out, load_ref,
+    field, buf, coef_a, coef_b, sums, loads, load_parts, own, line, packed, arrived, stage,
+    high, low, field_sems, recomb_sem,
     first_send, first_recv, first_own, line_send, line_recv, far_send, far_recv,
     back_send, back_recv, back_own, load_sems,
 ):
-    steps, group, cells_y, cells_x = zfirst.shape
+    steps, group, cells_y, cells_x = buf.shape
+    depth_all = steps * group
     size_y, size_x = high.shape
+    tiles = source_ref.shape[1]
+    edge = depth_all // tiles
+    per_tile = steps // tiles
+    pairs = len(growth)
+    bins_total = table_ref.shape[1]
     part = group // span_x
     rows = part * cells_y
     per = 128 // edge
     packs = packed.shape[1]
-    tiles_x = size_x // edge
     lane_blocks = size_x // 128
-    tiles = source_ref.shape[1]
     block = 128
     gx, gy = lax.axis_index("gx"), lax.axis_index("gy")
     level, w = gy // part, lax.rem(gy, part)
@@ -235,14 +170,22 @@
     every_peer(
         lambda i, j: pl.semaphore_signal(barrier, inc=1, device_id=at(i, j), device_id_type=MESH)
     )
-    for s in range(steps):
-        pltpu.make_async_copy(zfirst.at[s, me], place(own, s, gx, w), first_own.at[s]).start()
-    pl.semaphore_wait(barrier, span_x * span_y - 1)
+    fetches = field_sems.shape[0]
+    fetch_rows = cells_y // fetches
+
+    def fetch(n):
+        part_rows = pl.ds(n * fetch_rows, fetch_rows)
+        return pltpu.make_async_copy(
+            log_crit.at[:, part_rows], field.at[:, part_rows], field_sems.at[n]
+        )
+
+    for n in range(fetches):
+        fetch(n).start()
 
     def first(s):
         def act(i, j):
             pltpu.make_async_remote_copy(
-                src_ref=zfirst.at[s, i * part + j],
+                src_ref=buf.at[s, i * part + j],
                 dst_ref=place(own, s, gx, w),
                 send_sem=first_send.at[s],
                 recv_sem=first_recv.at[s],
@@ -251,6 +194,7 @@
             ).start()
 
         each_of_level(act)
+        pltpu.make_async_copy(buf.at[s, me], place(own, s, gx, w), first_own.at[s]).start()
 
     def send_back(s):
         def act(i, j):
@@ -287,11 +231,11 @@
         )
 
     def wait_others(sem, s):
-        some = zfirst.at[0, pl.ds(0, group - 1)]
+        some = buf.at[0, pl.ds(0, group - 1)]
         pltpu.make_async_copy(some, some, sem.at[s]).wait()
 
     def wait_own(sem, s):
-        one = zfirst.at[0, 0]
+        one = buf.at[0, 0]
         pltpu.make_async_copy(one, one, sem.at[s]).wait()
 
     def wait_plane(sem, s):
@@ -300,32 +244,89 @@
     def wait_packed(sem, s):
         pltpu.make_async_copy(packed.at[s], packed.at[s], sem.at[s]).wait()
 
-    own_load = pltpu.make_async_copy(loads.at[gy], load_parts.at[gy], load_sems.at[2])
-    own_load.start()
-
-    def send_load(n, carry):
-        j = lax.rem(gy + n, span_y)
-        pltpu.make_async_remote_copy(
-            src_ref=loads.at[j],
-            dst_ref=load_parts.at[gy],
-            send_sem=load_sems.at[0],
-            recv_sem=load_sems.at[1],
-            device_id=at(gx, j),
-            device_id_type=MESH,
-        ).start()
-        return carry
-
-    lax.fori_loop(1, span_y, send_load, 0)
-
-    def begin(s, carry):
-        first(s)
-        return carry
-
-    lax.fori_loop(0, steps, begin, 0)
+    def turn_in(t):
+        span = slice(t * edge, (t + 1) * edge)
+
+        def one(row, carry):
+            turned = field[:, row, span].T
+            buf[pl.ds(t * per_tile, per_tile), :, row, :] = turned.reshape(per_tile, group, cells_x)
+            return carry
+
+        lax.fori_loop(0, cells_y, one, 0, unroll=4)
+
+    def gather(t):
+        def one(row, carry):
+            kinds = lax.broadcasted_iota(jnp.int32, (bins_total, cells_x), 0)
+            onehot = jnp.where(kinds == bins_ref[t, pl.ds(row, 1), :], 1.0, 0.0)
+            rates = jnp.dot(
+                table_ref[...], onehot.astype(jnp.bfloat16), preferred_element_type=jnp.float32
+            )
+            rates = rates * live_ref[t, pl.ds(row // edge, 1), :]
+            upper, lower = rates[:pairs], rates[pairs:]
+            coef_a[:, row, :] = upper + lower
+            coef_b[:, row, :] = upper * rise_ref[1] + lower * rise_ref[0]
+            return carry
+
+        lax.fori_loop(0, cells_y, one, 0, unroll=4)
+        sums[t] = jnp.zeros(sums.shape[1:], jnp.float32)
+
+    def evaluate(s):
+        t = s // per_tile
+        batch = 4
+
+        def one(n, carry):
+            rows = pl.ds(pl.multiple_of(n // (group // batch) * 8, 8), 8)
+            planes = pl.ds(n % (group // batch) * batch, batch)
+            value = integral(
+                buf[s, planes, rows, :], growth,
+                lambda p: coef_a[p, rows, :], lambda p: coef_b[p, rows, :],
+            )
+            buf[s, planes, rows, :] = value
+            sums[t, rows, :] += jnp.sum(value, axis=0)
+            return carry
+
+        lax.fori_loop(0, cells_y // 8 * (group // batch), one, 0)
+
+    def turn_out(start, count):
+        def one(n, carry):
+            row = start + n
+            flat = buf[:, :, row, :].reshape(depth_all, cells_x)
+            field[:, row, :] = flat.T
+            return carry
+
+        lax.fori_loop(0, count, one, 0, unroll=2)
+
+    def send_loads():
+        blocks_y = live_ref.shape[1]
+        lines = [
+            jnp.sum(sums[t, b * edge : (b + 1) * edge, :], axis=0, keepdims=True)
+            for t in range(tiles)
+            for b in range(blocks_y)
+        ]
+        for g in range(span_y):
+            share_of = None
+            for n, line_sum in enumerate(lines):
+                chosen = jnp.where(route_ref[pl.ds(n, 1), :] == g, line_sum, 0.0)
+                share_of = chosen if share_of is None else share_of + chosen
+            total = jnp.sum(share_of, axis=1, keepdims=True) / (edge * edge * edge) / capacity
+            loads[g] = jnp.broadcast_to(total, (8, 128))
+        pltpu.make_async_copy(loads.at[gy], load_parts.at[gy], load_sems.at[2]).start()
+
+        def send(n, carry):
+            j = lax.rem(gy + n, span_y)
+            pltpu.make_async_remote_copy(
+                src_ref=loads.at[j],
+                dst_ref=load_parts.at[gy],
+                send_sem=load_sems.at[0],
+                recv_sem=load_sems.at[1],
+                device_id=at(gx, j),
+                device_id_type=MESH,
+            ).start()
+            return carry
+
+        lax.fori_loop(1, span_y, send, 0)
 
     lane = lax.broadcasted_iota(jnp.int32, (edge, 128), 1)
-    for r in range(per):
-        unpack_stage[r] = jnp.zeros((edge, 128), jnp.float32)
 
     def rows_at(start, count):
         return pl.ds(pl.multiple_of(start, count), count)
@@ -345,7 +346,7 @@
             return carry
 
         lax.fori_loop(0, rows // edge * lane_blocks, fill, 0)
-        t = s // (steps // tiles)
+        t = s // per_tile
 
         def one(g, carry):
             total = None
@@ -358,19 +359,21 @@
         lax.fori_loop(0, packs, one, 0)
 
     def unpack(s):
+        for r in range(per):
+            stage[r] = jnp.zeros((edge, 128), jnp.float32)
         def fill(g, carry):
             for r, value in enumerate(turns(arrived[s, g])):
-                unpack_stage[(g + 1) * per + r] = value
+                stage[(g + 1) * per + r] = value
             return carry
 
         lax.fori_loop(0, packs, fill, 0)
-        t = s // (steps // tiles)
+        t = s // per_tile
 
         def one(n, carry):
             down, block_x = n // lane_blocks, lax.rem(n, lane_blocks)
             total = None
             for q in range(per):
-                piece = unpack_stage[place_ref[1 - half, t, n * per + q]]
+                piece = stage[place_ref[1 - half, t, n * per + q]]
                 total = piece if total is None else jnp.where(lane >= q * edge, piece, total)
             to = (
                 rows_at((1 - half) * 2 * rows + down * edge, edge),
@@ -423,55 +426,74 @@
         lax.fori_loop(0, rows // block, for_me, 0)
         send_back(s)
 
-    ahead = min(2, steps - 1)
+    def end_first(s):
+        wait_own(first_own, s)
+        wait_others(first_recv, s)
+        to_mate(own, s).start()
+
+    def end_second(s):
+        wait_plane(line_recv, s)
+
+        def for_me(r, carry):
+            line[s, rows_at(r * block, block), :] = along_x(line[s, rows_at(r * block, block), :])
+            return carry
+
+        lax.fori_loop(0, rows // block, for_me, 0)
+        send_back(s)
+
+    last = 6
+    out_rounds = 4
+
+    def at_step(i, who, lag, act):
+        @pl.when(who & (i >= lag) & (i < steps + lag))
+        def _():
+            act(i - lag)
+
+    def body(i, carry):
+        for t in range(tiles):
+            @pl.when(i == t * per_tile)
+            def _():
+                if t == 0:
+                    for n in range(fetches):
+                        fetch(n).wait()
+                turn_in(t)
+                gather(t)
+
+        @pl.when(i < steps)
+        def _():
+            evaluate(i)
+
+        @pl.when(i == 0)
+        def _():
+            pl.semaphore_wait(barrier, span_x * span_y - 1)
+
+        @pl.when(i < steps)
+        def _():
+            first(i)
+
+        at_step(i, is_end, 1, end_first)
+        at_step(i, is_middle, 2, middle_first)
+        at_step(i, is_middle, 4, middle_second)
+        at_step(i, is_end, last, end_second)
+
+        @pl.when(i == steps)
+        def _():
+            send_loads()
+
+        @pl.when((i >= steps) & (i < steps + out_rounds))
+        def _():
+            turn_out((i - steps) * (cells_y // out_rounds), cells_y // out_rounds)
+
+        return carry
+
+    lax.fori_loop(0, steps + last, body, 0)
+    write = pltpu.make_async_copy(field, recomb, recomb_sem)
+    write.start()
 
     @pl.when(is_middle)
     def _():
-        def body(i, carry):
-            @pl.when(i < steps)
-            def _():
-                middle_first(i)
-
-            @pl.when(i >= ahead)
-            def _():
-                middle_second(i - ahead)
-
-            return carry
-
-        lax.fori_loop(0, steps + ahead, body, 0)
-
         def drain(s, carry):
             wait_packed(far_send, s)
-            wait_plane(line_send, s)
-            return carry
-
-        lax.fori_loop(0, steps, drain, 0)
-
-    @pl.when(is_end)
-    def _():
-        def feed(s, carry):
-            wait_own(first_own, s)
-            wait_others(first_recv, s)
-            to_mate(own, s).start()
-            return carry
-
-        lax.fori_loop(0, steps, feed, 0)
-
-        def body(s, carry):
-            wait_plane(line_recv, s)
-
-            def for_me(r, carry):
-                line[s, rows_at(r * block, block), :] = along_x(line[s, rows_at(r * block, block), :])
-                return carry
-
-            lax.fori_loop(0, rows // block, for_me, 0)
-            send_back(s)
-            return carry
-
-        lax.fori_loop(0, steps, body, 0)
-
-        def drain(s, carry):
-            wait_plane(line_send, s)
             return carry
 
         lax.fori_loop(0, steps, drain, 0)
@@ -479,9 +501,11 @@
     some_loads = loads.at[pl.ds(0, span_y - 1)]
     pltpu.make_async_copy(some_loads, some_loads, load_sems.at[0]).wait()
     pltpu.make_async_copy(some_loads, some_loads, load_sems.at[1]).wait()
-    own_load.wait()
+    pltpu.make_async_copy(loads.at[0], loads.at[0], load_sems.at[2]).wait()
+    load_ref[...] = jnp.sum(load_parts[...], axis=0)
 
     def finish(s, carry):
+        wait_plane(line_send, s)
         wait_others(first_send, s)
         wait_others(back_send, s)
         wait_own(back_own, s)
@@ -489,39 +513,57 @@
         return carry
 
     lax.fori_loop(0, steps, finish, 0)
+    write.wait()
 
 
 def exchange(
-    slots, collective, zfirst, loads, source, position, cy_high, cy_low, cx_high, cx_low, span_x,
-    span_y, edge,
+    slots, collective, span_x, span_y, growth, capacity, log_crit, bins, live, routes, table, rise,
+    source, position, cy_high, cy_low, cx_high, cx_low,
 ):
-    steps, group, cells_y, cells_x = zfirst.shape
+    cells_x, cells_y, depth_all = log_crit.shape
+    group = span_x * span_y // levels
+    steps = depth_all // group
+    edge = depth_all // source.shape[1]
     size_y, size_x = cy_high.shape[0], cx_high.shape[0]
     rows = size_y // levels
     packs = slots * edge // 128
+    per = 128 // edge
+    stage_size = max(2 * rows * size_x // edge // edge, per * (packs + 1))
     anywhere = pl.BlockSpec(memory_space=pl.ANY)
     inside = pl.BlockSpec(memory_space=pltpu.VMEM)
     scalars = pl.BlockSpec(memory_space=pltpu.SMEM)
     planes = pltpu.VMEM((steps, rows, size_x), jnp.float32)
     packing = pltpu.VMEM((steps, packs, edge, 128), jnp.float32)
+    coefs = pltpu.VMEM((len(growth), cells_y, cells_x), jnp.float32)
+    parts = pltpu.VMEM((span_y, 8, 128), jnp.float32)
+    halved = pltpu.VMEM((size_y, size_x), jnp.bfloat16)
     sems = pltpu.SemaphoreType.DMA((steps,))
     return pl.pallas_call(
-        functools.partial(exchange_kernel, span_x, span_y, edge),
-        in_specs=[anywhere] * 2 + [scalars] * 2 + [inside] * 4,
-        out_specs=[anywhere] * 2,
+        functools.partial(exchange_kernel, span_x, span_y, growth, capacity),
+        in_specs=[anywhere] + [inside] * 5 + [scalars] * 2 + [inside] * 4,
+        out_specs=[anywhere] * 2 + [inside],
         out_shape=[
-            jax.ShapeDtypeStruct(zfirst.shape, jnp.float32),
-            jax.ShapeDtypeStruct(loads.shape, jnp.float32),
+            jax.ShapeDtypeStruct(log_crit.shape, jnp.float32),
+            jax.ShapeDtypeStruct((steps, group, cells_y, cells_x), jnp.float32),
+            jax.ShapeDtypeStruct((8, 128), jnp.float32),
         ],
         scratch_shapes=[
+            pltpu.VMEM(log_crit.shape, jnp.float32),
+            pltpu.VMEM((steps, group, cells_y, cells_x), jnp.float32),
+            coefs,
+            coefs,
+            pltpu.VMEM((source.shape[1], cells_y, cells_x), jnp.float32),
+            parts,
+            parts,
             planes,
             planes,
             packing,
             packing,
-            pltpu.VMEM((2 * rows * size_x // edge // edge, edge, 128), jnp.float32),
-            pltpu.VMEM((128 // edge * (packs + 1), edge, 128), jnp.float32),
-            pltpu.VMEM((size_y, size_x), jnp.bfloat16),
-            pltpu.VMEM((size_y, size_x), jnp.bfloat16),
+            pltpu.VMEM((stage_size, edge, 128), jnp.float32),
+            halved,
+            halved,
+            pltpu.SemaphoreType.DMA((4,)),
+            pltpu.SemaphoreType.DMA,
         ]
         + [sems] * 10
         + [pltpu.SemaphoreType.DMA((3,))],
@@ -529,7 +571,10 @@
             collective_id=collective, has_side_effects=True, vmem_limit_bytes=vmem_grant
         ),
         name=f"exchange{slots}",
-    )(zfirst, loads, source, position, cy_high, cy_low, cx_high, cx_low)
+    )(
+        log_crit, bins, live, routes, table, rise, source, position, cy_high, cy_low, cx_high,
+        cx_low,
+    )
 
 
 def slot_tables(masks, edge):
@@ -607,27 +652,17 @@
     nodes = rate_table.shape[1]
     half = nodes // 2
 
-    bins = col_bins.transpose(1, 2, 0).reshape(cells_y * tiles, cells_x)
-    live = (tile_mask == 1).astype(jnp.float32).transpose(1, 2, 0)
-    live = jnp.broadcast_to(
-        live[:, None, :, :, None], (blocks_y, edge, tiles, blocks_x, edge)
-    ).reshape(cells_y * tiles, cells_x)
+    bins = col_bins.transpose(2, 1, 0)
+    live = jnp.repeat((tile_mask == 1).astype(jnp.float32).transpose(2, 1, 0), edge, axis=2)
+    routes = jnp.repeat(
+        tile_route.transpose(2, 1, 0).reshape(tiles * blocks_y, blocks_x), edge, axis=1
+    )
     table = jnp.concatenate([rate_table[:, half:], rate_table[:, half - 1 :: -1]], axis=1).T
 
-    recomb, zfirst, sums = evaluate(log_crit, bins, live, table, node_growth(nodes), tiles)
-
-    tile_means = jnp.sum(
-        sums.reshape(blocks_y, edge, tiles, blocks_x, edge), axis=(1, 4)
-    ) / (edge * edge * edge)
-    route = tile_route.transpose(1, 2, 0)
+    growth = node_growth(nodes)
+    ends = np.array([growth, [1.0 / e for e in growth]], np.float32)
+    rise = jnp.asarray(np.broadcast_to(ends[:, :, None], (2, half, cells_x)))
     capacity = blocks_x * blocks_y * tiles // 2
-    route_ids = jnp.arange(span_y, dtype=jnp.int32)
-    contribution = (
-        jnp.sum(
-            jnp.where(route[..., None] == route_ids, tile_means[..., None], 0.0), axis=(0, 1, 2)
-        )
-        / capacity
-    )
     table_x = wave_table(filt_x.shape[0])
     table_y = table_x if filt_y.shape == filt_x.shape else wave_table(filt_y.shape[0])
     mine = jnp.pad((tile_mask == 1).astype(jnp.int32).reshape(1, -1), ((0, 7), (0, 128 - blocks_x * blocks_y * tiles)))
@@ -637,21 +672,17 @@
     source, position, most = slot_tables(masks, edge)
     every = position.shape[2]
     few = every * 19 // 32
-    group = devices // levels
     operands = (
-        zfirst.reshape(depth_all // group, group, cells_y, cells_x),
-        jnp.broadcast_to(contribution[:, None, None], (span_y, 8, 128)),
-        source, position,
+        log_crit, bins, live, routes, table, rise, source, position,
         *outer_halves(circulant(filt_y, table_y)), *outer_halves(circulant(filt_x, table_x)),
     )
 
     def run(slots, collective):
-        return lambda *args: exchange(slots, collective, *args, span_x, span_y, edge)
-
-    back, load_parts = lax.cond(most <= few, run(few, 2), run(every, 3), *operands)
-    device_load = jnp.sum(load_parts[:, 0, 0])
+        return lambda *args: exchange(slots, collective, span_x, span_y, growth, capacity, *args)
+
+    recomb, back, device_load = lax.cond(most <= few, run(few, 2), run(every, 3), *operands)
     smoothed = turn(back.reshape(depth_all, cells_y, cells_x))
-    return (recomb, smoothed, device_load.reshape(1, 1))
+    return (recomb, smoothed, device_load[:1, :1])
 
 
 def solution(mesh):

time: 244 us -> 244 us (level)
  local copies, waits for them, and re-layouts: 7.43 us -> 12 us
  other arithmetic: 11.4 us -> 7.82 us
    unnamed x3 -> x4, local copies, waits for them, and re-layouts: 0.78 us -> 5.71 us
    pallas_call x2 -> x1, Pallas kernels: 197 us -> 197 us  [exchange(): pl.pallas_call(functools.partial(exchange_kernel, span_x, span_y, growth,...]
where the time goes in v2:
time: 244 us; the launch traced here: 243 us
  Pallas kernels  218 us (89%)
  local copies, waits for them, and re-layouts  12 us (5%)
  other arithmetic  7.82 us (3%)
  matrix products  3.91 us (2%)
    pallas_call x1, Pallas kernels, exchange(): pl.pallas_call(functools.partial(exchange_kernel, span_x, span_y, growth,...  197 us
    pallas_call x1, Pallas kernels, share(): pl.pallas_call(functools.partial(share_kernel, span_x, span_y), in_specs=...  12.5 us
    pallas_call x1, Pallas kernels, turn(): pl.pallas_call(turn_kernel, grid=(cells_y // rows,), in_specs=[pl.BlockSp...  8.44 us
    unnamed x4, local copies, waits for them, and re-layouts  5.71 us

profile of v2, /device:TPU:0, one launch (start us, length us, event | category | flops | bytes accessed | tf_op | source)
XLA Modules:
  0.0 243.4 jit_solution(4305478943661399179)
XLA Ops:
  0.7 0.8 slice.34
  1.4 0.8 slice.32
  2.2 0.8 fusion.27
  2.9 0.8 fusion.26
  3.7 0.8 copy.25
  4.5 0.7 convert_bitcast_fusion
  5.2 0.1 copy.24
  5.3 0.1 reshape.118
  5.3 0.6 pad_convert_fusion.mine
  5.9 0.1 broadcast_in_dim.56
  6.0 0.1 reshape.119
  6.1 0.1 broadcast_in_dim.57
  6.2 0.1 reshape.121
  6.3 0.7 fusion.32
  7.0 12.5 %share.1 = s32[32,8,128]{2,1,0:T(8,128)} custom-call(s32[8,128]{1,0:T(8,128)} %pad_convert_fusion.mine), custom_call_target="tpu_custom_call" | custom-call | tf_op jit(solution)/shard_map/share/pallas_call | solution.py:103
  19.5 0.9 slice.28
  20.4 0.1 copy.20
  20.5 0.1 reshape_squeeze.3
  20.6 0.3 copy.21
  20.9 0.2 reshape_reshape.3
  21.1 0.2 fusion.23
  21.2 0.6 reduce_max.9
  22.5 0.2 select_reduce_fusion
  22.8 0.9 copy.34
  23.7 3.8 %fusion.8 = f32[512,512]{1,0:T(8,128)S(1)} fusion(f32[512]{0:T(512)S(1)} %get-tuple-element.113, s32[512]{0:T(512)S(1)} %get-tuple-element.96), kind=kLoop, calls=%fused_computation.16 | loop fusion | flops 3932160 | bytes 1052672 | tf_op jit(solution)/shard_map/cos | solution.py:631
  27.5 0.0 copy-start
  27.5 0.3 broadcast_multiply_fusion
  27.8 1.9 fusion.1
  29.7 1.9 fusion.3
  31.6 0.0 copy-done
  31.6 0.1 jit_solution_.3
  31.7 198.5 %conditional.1 = (f32[128,64,128]{2,1,0:T(8,128)}, f32[16,8,64,128]{3,2,1,0:T(8,128)}, f32[1,1]{1,0:T(1,128)}) conditional(s32[]{:T(128)} %convert_element_type.26, (f32[128,64,128]{2,1,0:T(8,128)}, s32[4,64,128]{2,1,0:T(8,128)S(1)}, f32[4,2,128]{2,1,0:T(2,128)S(1)}, s32[8,128]{1,0:T(8,128)S(1)}, bf16[64,128]{1,0:T(8,128)(2,1)S(1)}, ...), branch_computations={%region_3.4_spmd, %region_4.5_spmd} | conditional | bytes 32 | solution.py:683
  31.9 197.1 %exchange76.1 = (f32[128,64,128]{2,1,0:T(8,128)}, f32[16,8,64,128]{3,2,1,0:T(8,128)}, f32[8,128]{1,0:T(8,128)}) custom-call(f32[128,64,128]{2,1,0:T(8,128)} %get-tuple-element.70.log_crit, s32[4,64,128]{2,1,0:T(8,128)S(1)} %get-tuple-element.71.bins_ref, f32[4,2,128]{2,1,0:T(2,128)S(1)} %get-tuple-element.72.live_ref, ...), custom_call_target="tpu_custom_call" | custom-call | tf_op jit(solution)/shard_map/cond/branch_1_fun/exchange76/pallas_call | solution.py:541
  229.0 1.2 slice.20
  230.2 8.4 %turn.1 = f32[128,64,128]{2,1,0:T(8,128)} custom-call(f32[128,64,128]{2,1,0:T(8,128)} %bitcast.34), custom_call_target="tpu_custom_call" | custom-call | tf_op jit(solution)/shard_map/turn/pallas_call | solution.py:608
  238.6 4.8 %copy.42 = f32[128,64,128]{2,1,0:T(8,128)} copy(f32[128,64,128]{2,1,0:T(8,128)} %get-tuple-element.123) | data formatting | bytes 8388608
  (7 shorter events, 0.1 us)
Async XLA Ops:
  27.5 4.1 %copy-start = (f32[2,32]{1,0:T(2,128)S(1)}, f32[2,32]{1,0:T(2,128)}, u32[]{:S(2)}) copy-start(f32[2,32]{1,0:T(2,128)} %constant.106.clone) | copy-start | bytes 772

commit v3 on v2

--- a/solution.py
+++ b/solution.py
@@ -115,7 +115,7 @@
     span_x, span_y, growth, capacity, log_crit, bins_ref, live_ref, route_ref, table_ref, rise_ref,
     source_ref, place_ref, cy_high, cy_low, cx_high, cx_low,
     recomb, out, load_ref,
-    field, buf, coef_a, coef_b, sums, loads, load_parts, own, line, packed, arrived, stage,
+    field, buf, known, coefs, sums, loads, load_parts, own, line, packed, arrived, stage,
     high, low, field_sems, recomb_sem,
     first_send, first_recv, first_own, line_send, line_recv, far_send, far_recv,
     back_send, back_recv, back_own, load_sems,
@@ -127,7 +127,6 @@
     edge = depth_all // tiles
     per_tile = steps // tiles
     pairs = len(growth)
-    bins_total = table_ref.shape[1]
     part = group // span_x
     rows = part * cells_y
     per = 128 // edge
@@ -244,30 +243,53 @@
     def wait_packed(sem, s):
         pltpu.make_async_copy(packed.at[s], packed.at[s], sem.at[s]).wait()
 
-    def turn_in(t):
-        span = slice(t * edge, (t + 1) * edge)
-
-        def one(row, carry):
-            turned = field[:, row, span].T
-            buf[pl.ds(t * per_tile, per_tile), :, row, :] = turned.reshape(per_tile, group, cells_x)
-            return carry
-
-        lax.fori_loop(0, cells_y, one, 0, unroll=4)
+    def unrolled(count, width, act):
+        def some(n, carry):
+            for r in range(width):
+                act(n * width + r)
+            return carry
+
+        lax.fori_loop(0, count // width, some, 0)
+        for n in range(count // width * width, count):
+            act(n)
+
+    def turned(value):
+        flat = jnp.swapaxes(value, 0, 1)
+        return jnp.swapaxes(jnp.stack([flat[r].T for r in range(8)]), 0, 1)
+
+    def eight(n):
+        return pl.ds(pl.multiple_of(n * 8, 8), 8)
+
+    def turn_in():
+        def one(n, carry):
+            value = turned(field[:, eight(n), :])
+            buf[:, :, eight(n), :] = value.reshape(steps, group, 8, cells_x)
+            return carry
+
+        lax.fori_loop(0, cells_y // 8, one, 0)
+
+    def turn_out(n):
+        value = buf[:, :, eight(n), :].reshape(depth_all, 8, cells_x)
+        field[:, eight(n), :] = turned(value)
+
+    def tabulate():
+        rates = table_ref[...].astype(jnp.float32)
+        upper, lower = rates[:pairs], rates[pairs:]
+        known[:pairs] = upper + lower
+        known[pairs:] = upper * rise_ref[1] + lower * rise_ref[0]
 
     def gather(t):
-        def one(row, carry):
-            kinds = lax.broadcasted_iota(jnp.int32, (bins_total, cells_x), 0)
-            onehot = jnp.where(kinds == bins_ref[t, pl.ds(row, 1), :], 1.0, 0.0)
-            rates = jnp.dot(
-                table_ref[...], onehot.astype(jnp.bfloat16), preferred_element_type=jnp.float32
-            )
-            rates = rates * live_ref[t, pl.ds(row // edge, 1), :]
-            upper, lower = rates[:pairs], rates[pairs:]
-            coef_a[:, row, :] = upper + lower
-            coef_b[:, row, :] = upper * rise_ref[1] + lower * rise_ref[0]
-            return carry
-
-        lax.fori_loop(0, cells_y, one, 0, unroll=4)
+        def one(n, carry):
+            kinds = bins_ref[t, eight(n), :]
+            live = jnp.broadcast_to(live_ref[t, pl.ds(n * 8 // edge, 1), :], kinds.shape)
+            for p in range(2 * pairs):
+                row = jnp.broadcast_to(known[pl.ds(p, 1), :], kinds.shape)
+                coefs[p, eight(n), :] = live * jnp.take_along_axis(
+                    row, kinds, axis=1, mode="promise_in_bounds"
+                )
+            return carry
+
+        lax.fori_loop(0, cells_y // 8, one, 0)
         sums[t] = jnp.zeros(sums.shape[1:], jnp.float32)
 
     def evaluate(s):
@@ -279,22 +301,13 @@
             planes = pl.ds(n % (group // batch) * batch, batch)
             value = integral(
                 buf[s, planes, rows, :], growth,
-                lambda p: coef_a[p, rows, :], lambda p: coef_b[p, rows, :],
+                lambda p: coefs[p, rows, :], lambda p: coefs[pairs + p, rows, :],
             )
             buf[s, planes, rows, :] = value
             sums[t, rows, :] += jnp.sum(value, axis=0)
             return carry
 
         lax.fori_loop(0, cells_y // 8 * (group // batch), one, 0)
-
-    def turn_out(start, count):
-        def one(n, carry):
-            row = start + n
-            flat = buf[:, :, row, :].reshape(depth_all, cells_x)
-            field[:, row, :] = flat.T
-            return carry
-
-        lax.fori_loop(0, count, one, 0, unroll=2)
 
     def send_loads():
         blocks_y = live_ref.shape[1]
@@ -335,41 +348,40 @@
         return [value if r == 0 else pltpu.roll(value, r * edge, 1) for r in range(per)]
 
     def pack(s):
-        def fill(n, carry):
-            down, across = n // lane_blocks, pl.ds(pl.multiple_of(n % lane_blocks * 128, 128), 128)
-            chunk = rows_at(down * edge, edge)
-            strip = rows // edge * lane_blocks
+        strip = rows // edge * lane_blocks
+
+        def fill(n):
+            across = pl.ds(pl.multiple_of(n % lane_blocks * 128, 128), 128)
+            chunk = rows_at(n // lane_blocks * edge, edge)
             for r, value in enumerate(turns(own[s, chunk, across])):
                 stage[(side * strip + n) * per + r] = value
             for r, value in enumerate(turns(line[s, chunk, across])):
                 stage[((1 - side) * strip + n) * per + r] = value
-            return carry
-
-        lax.fori_loop(0, rows // edge * lane_blocks, fill, 0)
+
+        unrolled(strip, 2, fill)
         t = s // per_tile
 
-        def one(g, carry):
+        def one(g):
             total = None
             for q in range(per):
                 piece = stage[source_ref[half, t, g * per + q]]
                 total = piece if total is None else jnp.where(lane >= q * edge, piece, total)
             packed[s, g] = total
-            return carry
-
-        lax.fori_loop(0, packs, one, 0)
+
+        unrolled(packs, 4, one)
 
     def unpack(s):
         for r in range(per):
             stage[r] = jnp.zeros((edge, 128), jnp.float32)
-        def fill(g, carry):
+
+        def fill(g):
             for r, value in enumerate(turns(arrived[s, g])):
                 stage[(g + 1) * per + r] = value
-            return carry
-
-        lax.fori_loop(0, packs, fill, 0)
+
+        unrolled(packs, 4, fill)
         t = s // per_tile
 
-        def one(n, carry):
+        def one(n):
             down, block_x = n // lane_blocks, lax.rem(n, lane_blocks)
             total = None
             for q in range(per):
@@ -380,9 +392,8 @@
                 rows_at(block_x * 128, 128),
             )
             high[to], low[to] = halves(total)
-            return carry
-
-        lax.fori_loop(0, 2 * rows // edge * lane_blocks, one, 0)
+
+        unrolled(2 * rows // edge * lane_blocks, 4, one)
 
     def split(source, s, which):
         def one(r, carry):
@@ -441,7 +452,7 @@
         lax.fori_loop(0, rows // block, for_me, 0)
         send_back(s)
 
-    last = 6
+    lags = (1, 2, 4, 6)
     out_rounds = 4
 
     def at_step(i, who, lag, act):
@@ -450,31 +461,23 @@
             act(i - lag)
 
     def body(i, carry):
-        for t in range(tiles):
-            @pl.when(i == t * per_tile)
-            def _():
-                if t == 0:
-                    for n in range(fetches):
-                        fetch(n).wait()
-                turn_in(t)
-                gather(t)
+        at_step(i, is_end, lags[0], end_first)
+
+        @pl.when((i < steps) & (i % per_tile == 0))
+        def _():
+            gather(i // per_tile)
 
         @pl.when(i < steps)
         def _():
             evaluate(i)
 
-        @pl.when(i == 0)
-        def _():
-            pl.semaphore_wait(barrier, span_x * span_y - 1)
-
         @pl.when(i < steps)
         def _():
             first(i)
 
-        at_step(i, is_end, 1, end_first)
-        at_step(i, is_middle, 2, middle_first)
-        at_step(i, is_middle, 4, middle_second)
-        at_step(i, is_end, last, end_second)
+        at_step(i, is_middle, lags[1], middle_first)
+        at_step(i, is_middle, lags[2], middle_second)
+        at_step(i, is_end, lags[3], end_second)
 
         @pl.when(i == steps)
         def _():
@@ -482,10 +485,17 @@
 
         @pl.when((i >= steps) & (i < steps + out_rounds))
         def _():
-            turn_out((i - steps) * (cells_y // out_rounds), cells_y // out_rounds)
+            for n in range(cells_y // 8 // out_rounds):
+                turn_out((i - steps) * (cells_y // 8 // out_rounds) + n)
 
         return carry
 
+    last = max(lags[3], out_rounds)
+    tabulate()
+    for n in range(fetches):
+        fetch(n).wait()
+    turn_in()
+    pl.semaphore_wait(barrier, span_x * span_y - 1)
     lax.fori_loop(0, steps + last, body, 0)
     write = pltpu.make_async_copy(field, recomb, recomb_sem)
     write.start()
@@ -534,7 +544,6 @@
     scalars = pl.BlockSpec(memory_space=pltpu.SMEM)
     planes = pltpu.VMEM((steps, rows, size_x), jnp.float32)
     packing = pltpu.VMEM((steps, packs, edge, 128), jnp.float32)
-    coefs = pltpu.VMEM((len(growth), cells_y, cells_x), jnp.float32)
     parts = pltpu.VMEM((span_y, 8, 128), jnp.float32)
     halved = pltpu.VMEM((size_y, size_x), jnp.bfloat16)
     sems = pltpu.SemaphoreType.DMA((steps,))
@@ -550,8 +559,8 @@
         scratch_shapes=[
             pltpu.VMEM(log_crit.shape, jnp.float32),
             pltpu.VMEM((steps, group, cells_y, cells_x), jnp.float32),
-            coefs,
-            coefs,
+            pltpu.VMEM(table.shape, jnp.float32),
+            pltpu.VMEM((2 * len(growth), cells_y, cells_x), jnp.float32),
             pltpu.VMEM((source.shape[1], cells_y, cells_x), jnp.float32),
             parts,
             parts,
@@ -661,7 +670,7 @@
 
     growth = node_growth(nodes)
     ends = np.array([growth, [1.0 / e for e in growth]], np.float32)
-    rise = jnp.asarray(np.broadcast_to(ends[:, :, None], (2, half, cells_x)))
+    rise = jnp.asarray(np.broadcast_to(ends[:, :, None], (2, half, table.shape[1])))
     capacity = blocks_x * blocks_y * tiles // 2
     table_x = wave_table(filt_x.shape[0])
     table_y = table_x if filt_y.shape == filt_x.shape else wave_table(filt_y.shape[0])

time: 244 us -> 212 us (0.87)
  Pallas kernels: 218 us -> 186 us
    pallas_call x1, Pallas kernels: 197 us -> 166 us  [exchange(): pl.pallas_call(functools.partial(exchange_kernel, span_x, span_y, growth,...]
where the time goes in v3:
time: 212 us
  Pallas kernels  186 us (88%)
  local copies, waits for them, and re-layouts  12 us (6%)
  other arithmetic  7.82 us (4%)
  matrix products  3.91 us (2%)
    pallas_call x1, Pallas kernels, exchange(): pl.pallas_call(functools.partial(exchange_kernel, span_x, span_y, growth,...  166 us
    pallas_call x1, Pallas kernels, share(): pl.pallas_call(functools.partial(share_kernel, span_x, span_y), in_specs=...  12.5 us
    pallas_call x1, Pallas kernels, turn(): pl.pallas_call(turn_kernel, grid=(cells_y // rows,), in_specs=[pl.BlockSp...  8.44 us
    unnamed x4, local copies, waits for them, and re-layouts  5.71 us

profile of v3, /device:TPU:0, one launch (start us, length us, event | category | flops | bytes accessed | tf_op | source)
XLA Modules:
  0.0 211.8 jit_solution(14801103204927102067)
XLA Ops:
  0.7 0.8 slice.34
  1.4 0.8 slice.32
  2.2 0.8 fusion.27
  2.9 0.8 fusion.26
  3.7 0.8 copy.25
  4.5 0.7 convert_bitcast_fusion
  5.2 0.1 copy.24
  5.3 0.1 reshape.118
  5.3 0.6 pad_convert_fusion.mine
  5.9 0.1 broadcast_in_dim.56
  6.0 0.1 reshape.119
  6.1 0.1 broadcast_in_dim.57
  6.2 0.1 reshape.121
  6.3 0.7 fusion.32
  7.0 12.5 %share.1 = s32[32,8,128]{2,1,0:T(8,128)} custom-call(s32[8,128]{1,0:T(8,128)} %pad_convert_fusion.mine), custom_call_target="tpu_custom_call" | custom-call | tf_op jit(solution)/shard_map/share/pallas_call | solution.py:103
  19.5 0.9 slice.28
  20.4 0.1 copy.20
  20.5 0.1 reshape_squeeze.3
  20.6 0.3 copy.21
  20.9 0.2 reshape_reshape.3
  21.1 0.2 fusion.23
  21.2 0.6 reduce_max.9
  22.5 0.2 select_reduce_fusion
  22.8 0.9 copy.34
  23.7 3.8 %fusion.8 = f32[512,512]{1,0:T(8,128)S(1)} fusion(f32[512]{0:T(512)S(1)} %get-tuple-element.113, s32[512]{0:T(512)S(1)} %get-tuple-element.96), kind=kLoop, calls=%fused_computation.16 | loop fusion | flops 3932160 | bytes 1052672 | tf_op jit(solution)/shard_map/cos | solution.py:640
  27.5 0.0 copy-start
  27.5 0.3 broadcast_multiply_fusion
  27.8 1.9 fusion.1
  29.7 1.9 fusion.3
  31.6 0.0 copy-done
  31.6 0.1 jit_solution_.3
  31.7 166.9 %conditional.1 = (f32[128,64,128]{2,1,0:T(8,128)}, f32[16,8,64,128]{3,2,1,0:T(8,128)}, f32[1,1]{1,0:T(1,128)}) conditional(s32[]{:T(128)} %convert_element_type.26, (f32[128,64,128]{2,1,0:T(8,128)}, s32[4,64,128]{2,1,0:T(8,128)S(1)}, f32[4,2,128]{2,1,0:T(2,128)S(1)}, s32[8,128]{1,0:T(8,128)S(1)}, bf16[64,128]{1,0:T(8,128)(2,1)S(1)}, ...), branch_computations={%region_3.4_spmd, %region_4.5_spmd} | conditional | bytes 32 | solution.py:692
  31.8 165.5 %exchange76.1 = (f32[128,64,128]{2,1,0:T(8,128)}, f32[16,8,64,128]{3,2,1,0:T(8,128)}, f32[8,128]{1,0:T(8,128)}) custom-call(f32[128,64,128]{2,1,0:T(8,128)} %get-tuple-element.70.log_crit, s32[4,64,128]{2,1,0:T(8,128)S(1)} %get-tuple-element.71.bins_ref, f32[4,2,128]{2,1,0:T(2,128)S(1)} %get-tuple-element.72.live_ref, ...), custom_call_target="tpu_custom_call" | custom-call | tf_op jit(solution)/shard_map/cond/branch_1_fun/exchange76/pallas_call | solution.py:550
  197.3 1.2 slice.20
  198.5 8.4 %turn.1 = f32[128,64,128]{2,1,0:T(8,128)} custom-call(f32[128,64,128]{2,1,0:T(8,128)} %bitcast.34), custom_call_target="tpu_custom_call" | custom-call | tf_op jit(solution)/shard_map/turn/pallas_call | solution.py:617
  207.0 4.8 %copy.42 = f32[128,64,128]{2,1,0:T(8,128)} copy(f32[128,64,128]{2,1,0:T(8,128)} %get-tuple-element.123) | data formatting | bytes 8388608
  (7 shorter events, 0.1 us)
Async XLA Ops:
  27.5 4.1 %copy-start = (f32[2,32]{1,0:T(2,128)S(1)}, f32[2,32]{1,0:T(2,128)}, u32[]{:S(2)}) copy-start(f32[2,32]{1,0:T(2,128)} %constant.106.clone) | copy-start | bytes 772

commit v4 on v3

--- a/solution.py
+++ b/solution.py
@@ -253,10 +253,6 @@
         for n in range(count // width * width, count):
             act(n)
 
-    def turned(value):
-        flat = jnp.swapaxes(value, 0, 1)
-        return jnp.swapaxes(jnp.stack([flat[r].T for r in range(8)]), 0, 1)
-
     def eight(n):
         return pl.ds(pl.multiple_of(n * 8, 8), 8)
 
@@ -452,7 +448,7 @@
         lax.fori_loop(0, rows // block, for_me, 0)
         send_back(s)
 
-    lags = (1, 2, 4, 6)
+    lags = (2, 3, 5, 7)
     out_rounds = 4
 
     def at_step(i, who, lag, act):
@@ -547,6 +543,11 @@
     parts = pltpu.VMEM((span_y, 8, 128), jnp.float32)
     halved = pltpu.VMEM((size_y, size_x), jnp.bfloat16)
     sems = pltpu.SemaphoreType.DMA((steps,))
+    plane_bytes = 4 * steps * rows * size_x
+    held = (
+        4 * plane_bytes + 8 * steps * slots * edge * edge + 4 * stage_size * edge * 128
+        + 12 * size_y * size_x + 8 * len(growth) * cells_y * cells_x
+    )
     return pl.pallas_call(
         functools.partial(exchange_kernel, span_x, span_y, growth, capacity),
         in_specs=[anywhere] + [inside] * 5 + [scalars] * 2 + [inside] * 4,
@@ -577,7 +578,8 @@
         + [sems] * 10
         + [pltpu.SemaphoreType.DMA((3,))],
         compiler_params=pltpu.CompilerParams(
-            collective_id=collective, has_side_effects=True, vmem_limit_bytes=vmem_grant
+            collective_id=collective, has_side_effects=True,
+            vmem_limit_bytes=min(held + held // 16 + 2 * 1024 * 1024, vmem_grant),
         ),
         name=f"exchange{slots}",
     )(
@@ -606,38 +608,44 @@
     return source, place, most
 
 
-def turn_kernel(source_ref, out_ref):
-    for row in range(source_ref.shape[1]):
-        out_ref[:, row, :] = source_ref[:, row, :].T
-
-
-def turn(source):
+def turned(value):
+    flat = jnp.swapaxes(value, 0, 1)
+    return jnp.swapaxes(jnp.stack([flat[r].T for r in range(8)]), 0, 1)
+
+
+def turn_kernel(source_ref, kept_ref, out_ref, kept_out):
+    for row in range(0, source_ref.shape[1], 8):
+        out_ref[:, row : row + 8, :] = turned(source_ref[:, row : row + 8, :])
+    kept_out[...] = kept_ref[...]
+
+
+def turn(source, kept):
     depth_all, cells_y, cells_x = source.shape
     rows = 8
+    planes = pl.BlockSpec((depth_all, rows, cells_x), lambda j: (0, j, 0))
+    cells = pl.BlockSpec((cells_x, rows, depth_all), lambda j: (0, j, 0))
+    shape = jax.ShapeDtypeStruct((cells_x, cells_y, depth_all), jnp.float32)
     return pl.pallas_call(
         turn_kernel,
         grid=(cells_y // rows,),
-        in_specs=[pl.BlockSpec((depth_all, rows, cells_x), lambda j: (0, j, 0))],
-        out_specs=pl.BlockSpec((cells_x, rows, depth_all), lambda j: (0, j, 0)),
-        out_shape=jax.ShapeDtypeStruct((cells_x, cells_y, depth_all), jnp.float32),
+        in_specs=[planes, cells],
+        out_specs=[cells, cells],
+        out_shape=[shape, shape],
+        compiler_params=pltpu.CompilerParams(vmem_limit_bytes=16 * 1024 * 1024),
         name="turn",
-    )(source)
+    )(source, kept)
 
 
 def wave_freq(length):
     half = length // 2
-    return jnp.concatenate(
-        [jnp.arange(half + 1, dtype=jnp.int32), jnp.arange(1, half, dtype=jnp.int32)]
-    )
+    return np.concatenate([np.arange(half + 1), np.arange(1, half)])
 
 
 def wave_table(length):
-    half = length // 2
-    indices = jnp.arange(length, dtype=jnp.int32)
+    indices = np.arange(length)
     turns = indices[:, None] * wave_freq(length)[None, :] % length
-    angles = 2.0 * math.pi / length * turns.astype(jnp.float32)
-    shift = jnp.where(indices < half + 1, 0.0, math.pi / 2)[None, :]
-    return lax.optimization_barrier(jnp.cos(angles - shift))
+    shift = np.where(indices < length // 2 + 1, 0.0, math.pi / 2)[None, :]
+    return jnp.asarray(np.cos(2.0 * math.pi / length * turns - shift), jnp.float32)
 
 
 def circulant(gain, table):
@@ -645,7 +653,7 @@
     half = length // 2
     freq = wave_freq(length)
     weight = jnp.concatenate([gain[: half + 1], gain[1:half]])
-    doubled = jnp.where((freq == 0) | (freq == half), 1.0, 2.0).astype(jnp.float32)
+    doubled = jnp.asarray(np.where((freq == 0) | (freq == half), 1.0, 2.0), jnp.float32)
     scaled = lax.optimization_barrier(table * (weight * doubled / length))
     return lax.dot_general(
         scaled, table, (((1,), (1,)), ((), ())), precision=lax.Precision.HIGHEST
@@ -690,7 +698,7 @@
         return lambda *args: exchange(slots, collective, span_x, span_y, growth, capacity, *args)
 
     recomb, back, device_load = lax.cond(most <= few, run(few, 2), run(every, 3), *operands)
-    smoothed = turn(back.reshape(depth_all, cells_y, cells_x))
+    smoothed, recomb = turn(back.reshape(depth_all, cells_y, cells_x), recomb)
     return (recomb, smoothed, device_load[:1, :1])
 
 

time: 212 us -> 184 us (0.87)
  Pallas kernels: 186 us -> 166 us
  local copies, waits for them, and re-layouts: 12 us -> 7.39 us
  other arithmetic: 7.82 us -> 4.65 us
    pallas_call x1, Pallas kernels: 166 us -> 148 us  [exchange(): pl.pallas_call(functools.partial(exchange_kernel, span_x, span_y, growth,...]
    unnamed x4, local copies, waits for them, and re-layouts: 5.71 us -> 1.7 us
    cos x1 -> x0, other arithmetic: 3.82 us -> none  [wave_table(): return lax.optimization_barrier(jnp.cos(angles - shift))]
    pallas_call x1, Pallas kernels: 8.44 us -> 5.59 us  [turn(): pl.pallas_call(turn_kernel, grid=(cells_y // rows,), in_specs=[planes, ce...]
where the time goes in v4:
time: 184 us
  Pallas kernels  166 us (90%)
  local copies, waits for them, and re-layouts  7.39 us (4%)
  other arithmetic  4.65 us (3%)
  matrix products  3.89 us (2%)
    pallas_call x1, Pallas kernels, exchange(): pl.pallas_call(functools.partial(exchange_kernel, span_x, span_y, growth,...  148 us
    pallas_call x1, Pallas kernels, share(): pl.pallas_call(functools.partial(share_kernel, span_x, span_y), in_specs=...  12.5 us
    pallas_call x1, Pallas kernels, turn(): pl.pallas_call(turn_kernel, grid=(cells_y // rows,), in_specs=[planes, ce...  5.59 us
    dot_general x2, matrix products, circulant(): lax.dot_general(scaled, table, (((1,), (1,)), ((), ())), precision=lax.Pr...  3.75 us

profile of v4, /device:TPU:0, one launch (start us, length us, event | category | flops | bytes accessed | tf_op | source)
XLA Modules:
  0.0 183.6 jit_solution(8710817567448463455)
XLA Ops:
  0.6 0.0 copy-start
  0.7 0.8 slice.33
  1.5 0.8 slice.31
  2.3 0.8 fusion.31
  3.1 0.8 copy.46
  3.8 0.7 convert_bitcast_fusion
  4.5 0.1 reshape.49
  4.6 0.6 pad_convert_fusion.mine
  5.2 0.7 fusion.35
  6.0 12.5 %share.1 = s32[32,8,128]{2,1,0:T(8,128)} custom-call(s32[8,128]{1,0:T(8,128)} %pad_convert_fusion.mine), custom_call_target="tpu_custom_call" | custom-call | tf_op jit(solution)/shard_map/share/pallas_call | solution.py:103
  18.5 0.9 slice.27
  19.4 0.1 copy.42
  19.5 0.1 reshape_squeeze.3
  19.6 0.3 copy.43
  19.9 0.2 reshape_reshape.3
  20.0 0.1 bitcast_reduce_fusion
  20.2 0.6 reduce_max.9
  21.5 0.1 fusion.29
  21.6 0.9 copy.58
  22.6 1.5 broadcast_multiply_fusion
  24.1 0.0 copy-done
  24.1 1.9 %fusion.19 = (bf16[512,512]{1,0:T(8,128)(2,1)S(1)}, bf16[512,512]{1,0:T(8,128)(2,1)S(1)}) fusion(f32[512,512]{1,0:T(8,128)S(1)} %get-tuple-element.552, f32[512,512]{1,0:T(8,128)S(1)} %copy-done), kind=kOutput, calls=%fused_computation.42 | convolution fusion | flops 1611923456 | bytes 3145728 | tf_op jit(solution)/shard_map/dot_general | solution.py:658
  26.0 1.9 %fusion.21 = (bf16[512,512]{1,0:T(8,128)(2,1)S(1)}, bf16[512,512]{1,0:T(8,128)(2,1)S(1)}) fusion(f32[512,512]{1,0:T(8,128)S(1)} %get-tuple-element.551, f32[512,512]{1,0:T(8,128)S(1)} %copy-done), kind=kOutput, calls=%fused_computation.44 | convolution fusion | flops 1611923456 | bytes 3145728 | tf_op jit(solution)/shard_map/dot_general | solution.py:658
  27.9 150.1 %conditional.1 = (f32[128,64,128]{2,1,0:T(8,128)S(1)}, f32[128,64,128]{2,1,0:T(8,128)S(1)}, f32[1,1]{1,0:T(1,128)}) conditional(s32[]{:T(128)} %convert_element_type.23, (f32[128,64,128]{2,1,0:T(8,128)}, s32[4,64,128]{2,1,0:T(8,128)S(1)}, f32[4,2,4]{0,2,1:T(4,128)S(1)}, s32[4,2,4]{2,1,0:T(2,128)S(1)}, bf16[64,128]{1,0:T(8,128)(2,1)S(1)}, ...), branch_computations={%region_3.4_spmd.clone, %region_4.5_spmd.clone} | conditional | flops 417536 | bytes 695216 | solution.py:700
  28.0 0.2 select_reduce_fusion.1.source_ref
  28.2 0.1 copy.48
  28.3 0.1 broadcast_in_dim.56
  28.4 0.1 reshape.67.live_ref
  28.5 0.1 broadcast_in_dim.57
  28.6 0.1 reshape.68.route_ref
  28.6 0.8 jit_solution_.7.rise_ref
  29.4 148.1 %exchange76.1 = (f32[128,64,128]{2,1,0:T(8,128)S(1)}, f32[16,8,64,128]{3,2,1,0:T(8,128)S(1)}, f32[8,128]{1,0:T(8,128)S(1)}) custom-call(f32[128,64,128]{2,1,0:T(8,128)} %get-tuple-element.383.log_crit, s32[4,64,128]{2,1,0:T(8,128)S(1)} %get-tuple-element.371.bins_ref, f32[4,2,128]{2,1,0:T(2,128)S(1)} %reshape.67.live_ref, s32[8,128]{1,0:T(8,128)S(1)} %reshape.68.route_ref, ...), custom_call_target="tpu_custom_call" | custom-call | tf_op jit(solution)/shard_map/cond/branch_1_fun/exchange76/pallas_call | solution.py:551
  177.5 0.5 slice.38
  178.0 5.6 %turn.1 = (f32[128,64,128]{2,1,0:T(8,128)}, f32[128,64,128]{2,1,0:T(8,128)}) custom-call(f32[128,64,128]{2,1,0:T(8,128)S(1)} %get-tuple-element.103.source_ref, f32[128,64,128]{2,1,0:T(8,128)S(1)} %get-tuple-element.93.kept_ref), custom_call_target="tpu_custom_call" | custom-call | tf_op jit(solution)/shard_map/turn/pallas_call | solution.py:628
  (17 shorter events, 0.2 us)
Async XLA Ops:
  0.6 23.5 %copy-start = (f32[512,512]{1,0:T(8,128)S(1)}, f32[512,512]{1,0:T(8,128)}, u32[]{:S(2)}) copy-start(f32[512,512]{1,0:T(8,128)} %constant.81.clone) | copy-start | bytes 3145732

commit v5 on v4

--- a/solution.py
+++ b/solution.py
@@ -61,69 +61,19 @@
     return dot(a_high, b_high) + (dot(a_high, b_low) + dot(a_low, b_high))
 
 
-def share_kernel(span_x, span_y, mine, out, send_sem, recv_sem, own_sem):
-    devices = span_x * span_y
-    gx, gy = lax.axis_index("gx"), lax.axis_index("gy")
-    me = gx * span_y + gy
-
-    def each_peer(act):
-        def body(n, carry):
-            i = lax.rem(gx + n // span_y, span_x)
-            j = lax.rem(gy + n % span_y, span_y)
-            act({"gx": i, "gy": j})
-            return carry
-
-        lax.fori_loop(1, devices, body, 0)
-
-    barrier = pltpu.get_barrier_semaphore()
-    each_peer(lambda peer: pl.semaphore_signal(barrier, inc=1, device_id=peer, device_id_type=MESH))
-    own = pltpu.make_async_copy(mine, out.at[me], own_sem)
-    own.start()
-    pl.semaphore_wait(barrier, devices - 1)
-
-    def send(peer):
-        pltpu.make_async_remote_copy(
-            src_ref=mine,
-            dst_ref=out.at[me],
-            send_sem=send_sem,
-            recv_sem=recv_sem,
-            device_id=peer,
-            device_id_type=MESH,
-        ).start()
-
-    each_peer(send)
-    own.wait()
-    some = out.at[pl.ds(0, devices - 1)]
-    pltpu.make_async_copy(some, some, send_sem).wait()
-    pltpu.make_async_copy(some, some, recv_sem).wait()
-
-
-def share(mine, span_x, span_y):
-    inside = pl.BlockSpec(memory_space=pltpu.VMEM)
-    return pl.pallas_call(
-        functools.partial(share_kernel, span_x, span_y),
-        in_specs=[inside],
-        out_specs=inside,
-        out_shape=jax.ShapeDtypeStruct((span_x * span_y,) + mine.shape, mine.dtype),
-        scratch_shapes=[pltpu.SemaphoreType.DMA] * 3,
-        compiler_params=pltpu.CompilerParams(collective_id=1, has_side_effects=True),
-        name="share",
-    )(mine)
-
-
 def exchange_kernel(
     span_x, span_y, growth, capacity, log_crit, bins_ref, live_ref, route_ref, table_ref, rise_ref,
-    source_ref, place_ref, cy_high, cy_low, cx_high, cx_low,
-    recomb, out, load_ref,
+    mask_ref, cy_high, cy_low, cx_high, cx_low,
+    recomb, out, load_ref, most_ref,
     field, buf, known, coefs, sums, loads, load_parts, own, line, packed, arrived, stage,
-    high, low, field_sems, recomb_sem,
+    high, low, masks, made, source_ref, place_ref, field_sems, recomb_sem, mask_sems,
     first_send, first_recv, first_own, line_send, line_recv, far_send, far_recv,
     back_send, back_recv, back_own, load_sems,
 ):
     steps, group, cells_y, cells_x = buf.shape
     depth_all = steps * group
     size_y, size_x = high.shape
-    tiles = source_ref.shape[1]
+    tiles = bins_ref.shape[0]
     edge = depth_all // tiles
     per_tile = steps // tiles
     pairs = len(growth)
@@ -181,6 +131,70 @@
     for n in range(fetches):
         fetch(n).start()
 
+    me_all = gx * span_y + gy
+
+    def send_mask(i, j):
+        pltpu.make_async_remote_copy(
+            src_ref=mask_ref,
+            dst_ref=masks.at[me_all],
+            send_sem=mask_sems.at[0],
+            recv_sem=mask_sems.at[1],
+            device_id=at(i, j),
+            device_id_type=MESH,
+        ).start()
+
+    def tables():
+        some = masks.at[pl.ds(0, span_x * span_y - 1)]
+        pltpu.make_async_copy(some, some, mask_sems.at[0]).wait()
+        pltpu.make_async_copy(some, some, mask_sems.at[1]).wait()
+        pltpu.make_async_copy(mask_ref, mask_ref, mask_sems.at[2]).wait()
+        blocks_y, blocks_x = live_ref.shape[1], cells_x // edge
+        slots = source_ref.shape[1]
+        across = size_x // edge
+
+        def numbers(shape, axis):
+            return lax.broadcasted_iota(jnp.int32, shape, axis)
+
+        flags = masks[:, 0, :].astype(jnp.bfloat16)
+        held = jnp.zeros((slots, 128), jnp.float32)
+        slot = numbers((slots, 128), 0)
+        column = numbers((slots, 128), 1)
+        down, over = slot // across, slot % across
+        lane_of = (over % blocks_x * blocks_y + down % blocks_y) * tiles
+        owner = numbers((slots, span_x * span_y), 0)
+        owner = owner % across // blocks_x * span_y + owner // across // blocks_y
+        device = numbers((slots, span_x * span_y), 1)
+        for h in range(2):
+            chosen = jnp.where(owner + h * (span_y // 2) == device, 1.0, 0.0).astype(jnp.bfloat16)
+            picked = jnp.dot(chosen, flags, preferred_element_type=jnp.float32)
+            for t in range(tiles):
+                value = jnp.sum(
+                    jnp.where(column == lane_of + t, picked, 0.0), axis=1, keepdims=True
+                )
+                held = jnp.where(column == h * tiles + t, value, held)
+        later = numbers((slots, slots), 0) > numbers((slots, slots), 1)
+        before = jnp.where(later, 1.0, 0.0).astype(jnp.bfloat16)
+        rank = jnp.dot(before, held.astype(jnp.bfloat16), preferred_element_type=jnp.float32)
+        rank = rank.astype(jnp.int32)
+        live = held > 0.5
+        shift = (slot % per + per - rank % per) % per
+        places = jnp.where(live, (rank // per + 1) * per + shift, 0)
+        made[1] = places.T[: 2 * tiles]
+        rank = jnp.where(live, rank, -1)
+        to = numbers((slots, slots), 1)
+        origin = numbers((slots, slots), 0)
+        origin = origin // per * per + (to % per + per - origin % per) % per
+        for e in range(2 * tiles):
+            made[0, e : e + 1] = jnp.sum(
+                jnp.where(rank[:, e : e + 1] == to, origin, 0), axis=0, keepdims=True
+            )
+        most = jnp.max(jnp.sum(held, axis=0, keepdims=True), axis=1, keepdims=True)
+        most_ref[...] = jnp.broadcast_to(most, (8, 128))
+        for n, table in enumerate((source_ref, place_ref)):
+            copy = pltpu.make_async_copy(made.at[n], table, mask_sems.at[3 + n])
+            copy.start()
+            copy.wait()
+
     def first(s):
         def act(i, j):
             pltpu.make_async_remote_copy(
@@ -343,6 +357,9 @@
     def turns(value):
         return [value if r == 0 else pltpu.roll(value, r * edge, 1) for r in range(per)]
 
+    def inside(index):
+        return jnp.clip(index, 0, stage.shape[0] - 1)
+
     def pack(s):
         strip = rows // edge * lane_blocks
 
@@ -360,7 +377,7 @@
         def one(g):
             total = None
             for q in range(per):
-                piece = stage[source_ref[half, t, g * per + q]]
+                piece = stage[inside(source_ref[half * tiles + t, g * per + q])]
                 total = piece if total is None else jnp.where(lane >= q * edge, piece, total)
             packed[s, g] = total
 
@@ -381,7 +398,7 @@
             down, block_x = n // lane_blocks, lax.rem(n, lane_blocks)
             total = None
             for q in range(per):
-                piece = stage[place_ref[1 - half, t, n * per + q]]
+                piece = stage[inside(place_ref[(1 - half) * tiles + t, n * per + q])]
                 total = piece if total is None else jnp.where(lane >= q * edge, piece, total)
             to = (
                 rows_at((1 - half) * 2 * rows + down * edge, edge),
@@ -471,6 +488,10 @@
         def _():
             first(i)
 
+        @pl.when(i == 1)
+        def _():
+            tables()
+
         at_step(i, is_middle, lags[1], middle_first)
         at_step(i, is_middle, lags[2], middle_second)
         at_step(i, is_end, lags[3], end_second)
@@ -491,7 +512,9 @@
     for n in range(fetches):
         fetch(n).wait()
     turn_in()
+    pltpu.make_async_copy(mask_ref, masks.at[me_all], mask_sems.at[2]).start()
     pl.semaphore_wait(barrier, span_x * span_y - 1)
+    every_peer(send_mask)
     lax.fori_loop(0, steps + last, body, 0)
     write = pltpu.make_async_copy(field, recomb, recomb_sem)
     write.start()
@@ -524,20 +547,20 @@
 
 def exchange(
     slots, collective, span_x, span_y, growth, capacity, log_crit, bins, live, routes, table, rise,
-    source, position, cy_high, cy_low, cx_high, cx_low,
+    mask, cy_high, cy_low, cx_high, cx_low,
 ):
     cells_x, cells_y, depth_all = log_crit.shape
     group = span_x * span_y // levels
     steps = depth_all // group
-    edge = depth_all // source.shape[1]
+    edge = depth_all // bins.shape[0]
     size_y, size_x = cy_high.shape[0], cx_high.shape[0]
     rows = size_y // levels
     packs = slots * edge // 128
     per = 128 // edge
+    every = size_y // 2 // edge * (size_x // edge)
     stage_size = max(2 * rows * size_x // edge // edge, per * (packs + 1))
     anywhere = pl.BlockSpec(memory_space=pl.ANY)
     inside = pl.BlockSpec(memory_space=pltpu.VMEM)
-    scalars = pl.BlockSpec(memory_space=pltpu.SMEM)
     planes = pltpu.VMEM((steps, rows, size_x), jnp.float32)
     packing = pltpu.VMEM((steps, packs, edge, 128), jnp.float32)
     parts = pltpu.VMEM((span_y, 8, 128), jnp.float32)
@@ -550,11 +573,12 @@
     )
     return pl.pallas_call(
         functools.partial(exchange_kernel, span_x, span_y, growth, capacity),
-        in_specs=[anywhere] + [inside] * 5 + [scalars] * 2 + [inside] * 4,
-        out_specs=[anywhere] * 2 + [inside],
+        in_specs=[anywhere] + [inside] * 10,
+        out_specs=[anywhere] * 2 + [inside] * 2,
         out_shape=[
             jax.ShapeDtypeStruct(log_crit.shape, jnp.float32),
             jax.ShapeDtypeStruct((steps, group, cells_y, cells_x), jnp.float32),
+            jax.ShapeDtypeStruct((8, 128), jnp.float32),
             jax.ShapeDtypeStruct((8, 128), jnp.float32),
         ],
         scratch_shapes=[
@@ -562,7 +586,7 @@
             pltpu.VMEM((steps, group, cells_y, cells_x), jnp.float32),
             pltpu.VMEM(table.shape, jnp.float32),
             pltpu.VMEM((2 * len(growth), cells_y, cells_x), jnp.float32),
-            pltpu.VMEM((source.shape[1], cells_y, cells_x), jnp.float32),
+            pltpu.VMEM((bins.shape[0], cells_y, cells_x), jnp.float32),
             parts,
             parts,
             planes,
@@ -572,8 +596,13 @@
             pltpu.VMEM((stage_size, edge, 128), jnp.float32),
             halved,
             halved,
+            pltpu.VMEM((span_x * span_y, 8, 128), jnp.float32),
+            pltpu.VMEM((2, 2 * bins.shape[0], every), jnp.int32),
+            pltpu.SMEM((2 * bins.shape[0], every), jnp.int32),
+            pltpu.SMEM((2 * bins.shape[0], every), jnp.int32),
             pltpu.SemaphoreType.DMA((4,)),
             pltpu.SemaphoreType.DMA,
+            pltpu.SemaphoreType.DMA((5,)),
         ]
         + [sems] * 10
         + [pltpu.SemaphoreType.DMA((3,))],
@@ -583,29 +612,8 @@
         ),
         name=f"exchange{slots}",
     )(
-        log_crit, bins, live, routes, table, rise, source, position, cy_high, cy_low, cx_high,
-        cx_low,
-    )
-
-
-def slot_tables(masks, edge):
-    halves_count = 2
-    flat = masks.reshape(halves_count, -1, masks.shape[2]).transpose(0, 2, 1)
-    slots = flat.shape[2]
-    before = jnp.triu(jnp.ones((slots, slots), jnp.bfloat16), 1)
-    rank = jnp.dot(flat.astype(jnp.bfloat16), before, preferred_element_type=jnp.float32)
-    rank = rank.astype(jnp.int32)
-    per = 128 // edge
-    indices = jnp.arange(slots, dtype=jnp.int32)
-    shifted = (indices % per - rank) % per
-    position = jnp.where(flat == 1, rank, -1)
-    place = jnp.where(flat == 1, (rank // per + 1) * per + shifted, 0)
-    from_place = indices // per * per + (rank - indices) % per
-    source = jnp.sum(
-        jnp.where(position[:, :, None, :] == indices[:, None], from_place[:, :, None, :], 0), axis=3
-    )
-    most = jnp.max(jnp.sum(flat, axis=2))
-    return source, place, most
+        log_crit, bins, live, routes, table, rise, mask, cy_high, cy_low, cx_high, cx_low,
+    )
 
 
 def turned(value):
@@ -682,23 +690,25 @@
     capacity = blocks_x * blocks_y * tiles // 2
     table_x = wave_table(filt_x.shape[0])
     table_y = table_x if filt_y.shape == filt_x.shape else wave_table(filt_y.shape[0])
-    mine = jnp.pad((tile_mask == 1).astype(jnp.int32).reshape(1, -1), ((0, 7), (0, 128 - blocks_x * blocks_y * tiles)))
-    masks = share(mine, span_x, span_y)[:, 0, : blocks_x * blocks_y * tiles]
-    masks = masks.reshape(span_x, span_y, blocks_x, blocks_y, tiles).transpose(1, 3, 0, 2, 4)
-    masks = masks.reshape(span_y * blocks_y, span_x * blocks_x, tiles)
-    source, position, most = slot_tables(masks, edge)
-    every = position.shape[2]
+    mask = (tile_mask == 1).astype(jnp.float32).reshape(1, -1)
+    mask = jnp.pad(mask, ((0, 7), (0, 128 - mask.shape[1])))
+    every = span_y * blocks_y // 2 * span_x * blocks_x
     few = every * 19 // 32
     operands = (
-        log_crit, bins, live, routes, table, rise, source, position,
+        log_crit, bins, live, routes, table, rise, mask,
         *outer_halves(circulant(filt_y, table_y)), *outer_halves(circulant(filt_x, table_x)),
     )
 
     def run(slots, collective):
-        return lambda *args: exchange(slots, collective, span_x, span_y, growth, capacity, *args)
-
-    recomb, back, device_load = lax.cond(most <= few, run(few, 2), run(every, 3), *operands)
-    smoothed, recomb = turn(back.reshape(depth_all, cells_y, cells_x), recomb)
+        return exchange(slots, collective, span_x, span_y, growth, capacity, *operands)
+
+    def finish(planes, recomb):
+        return turn(planes.reshape(depth_all, cells_y, cells_x), recomb)
+
+    recomb, back, device_load, most = run(few, 2)
+    smoothed, recomb = lax.cond(
+        most[0, 0] <= few, finish, lambda planes, cells: finish(run(every, 3)[1], cells), back, recomb
+    )
     return (recomb, smoothed, device_load[:1, :1])
 
 

time: 184 us -> 171 us (0.929)
  Pallas kernels: 166 us -> 156 us
    pallas_call x1 -> x0, Pallas kernels: 12.5 us -> none  [share(): pl.pallas_call(functools.partial(share_kernel, span_x, span_y), in_specs=...]
    pallas_call x1, Pallas kernels: 5.59 us -> 7.75 us  [turn(): pl.pallas_call(turn_kernel, grid=(cells_y // rows,), in_specs=[planes, ce...]
where the time goes in v5:
time: 171 us; the launch traced here: 170 us
  Pallas kernels  156 us (91%)
  local copies, waits for them, and re-layouts  5.67 us (3%)
  matrix products  3.78 us (2%)
  other arithmetic  3.12 us (2%)
    pallas_call x1, Pallas kernels, exchange(): pl.pallas_call(functools.partial(exchange_kernel, span_x, span_y, growth,...  148 us
    pallas_call x1, Pallas kernels, turn(): pl.pallas_call(turn_kernel, grid=(cells_y // rows,), in_specs=[planes, ce...  7.75 us
    dot_general x2, matrix products, circulant(): lax.dot_general(scaled, table, (((1,), (1,)), ((), ())), precision=lax.Pr...  3.78 us

profile of v5, /device:TPU:0, one launch (start us, length us, event | category | flops | bytes accessed | tf_op | source)
XLA Modules:
  0.0 170.4 jit_solution(1190470192222091401)
XLA Ops:
  0.6 0.0 copy-start.1
  0.6 0.8 slice.29
  1.5 0.8 slice.27
  2.2 0.8 fusion.5
  3.0 0.8 copy.16
  3.8 0.7 compare_convert_fusion
  4.5 0.1 reshape.33
  4.6 0.1 copy.15
  4.7 0.1 broadcast_in_dim.8
  4.8 0.1 reshape.30.live_ref
  4.9 0.1 broadcast_in_dim.9
  4.9 0.1 reshape.32.route_ref
  5.0 0.7 fusion.7
  5.8 0.9 copy.18
  6.7 0.0 copy-start.2
  6.7 0.0 copy-start
  6.7 1.6 broadcast_multiply_fusion
  8.4 0.0 copy-done.1
  8.4 1.9 %fusion.1 = (bf16[512,512]{1,0:T(8,128)(2,1)S(1)}, bf16[512,512]{1,0:T(8,128)(2,1)S(1)}) fusion(f32[512,512]{1,0:T(8,128)S(1)} %get-tuple-element.61, f32[512,512]{1,0:T(8,128)S(1)} %copy-done.1), kind=kOutput, calls=%fused_computation.5 | convolution fusion | flops 1611923456 | bytes 3145728 | tf_op jit(solution)/shard_map/dot_general | solution.py:666
  10.3 1.9 %fusion.3 = (bf16[512,512]{1,0:T(8,128)(2,1)S(1)}, bf16[512,512]{1,0:T(8,128)(2,1)S(1)}) fusion(f32[512,512]{1,0:T(8,128)S(1)} %get-tuple-element.60, f32[512,512]{1,0:T(8,128)S(1)} %copy-done.1), kind=kOutput, calls=%fused_computation.7 | convolution fusion | flops 1611923456 | bytes 3145728 | tf_op jit(solution)/shard_map/dot_general | solution.py:666
  12.2 0.0 copy-done.2
  12.2 0.1 jit_solution_.3.rise_ref
  12.2 0.0 copy-done
  12.2 148.5 %exchange76.1 = (f32[128,64,128]{2,1,0:T(8,128)S(1)}, f32[16,8,64,128]{3,2,1,0:T(8,128)}, f32[8,128]{1,0:T(8,128)S(1)}, f32[8,128]{1,0:T(8,128)S(1)}) custom-call(f32[128,64,128]{2,1,0:T(8,128)S(1)} %copy-done, s32[4,64,128]{2,1,0:T(8,128)S(1)} %bitcast.20, f32[4,2,128]{2,1,0:T(2,128)S(1)} %reshape.30.live_ref, s32[8,128]{1,0:T(8,128)S(1)} %reshape.32.route_ref, ...), custom_call_target="tpu_custom_call" | custom-call | tf_op jit(solution)/shard_map/exchange76/pallas_call | solution.py:574
  160.7 0.5 slice.31
  161.3 0.5 slice.30
  162.4 8.0 %conditional.1 = ((f32[128,64,128]{2,1,0:T(8,128)}, f32[128,64,128]{2,1,0:T(8,128)})) conditional(s32[]{:T(128)} %bitcast.7, (f32[128,64,128]{2,1,0:T(8,128)S(1)}, s32[4,64,128]{2,1,0:T(8,128)S(1)}, f32[4,2,128]{2,1,0:T(2,128)S(1)}, s32[8,128]{1,0:T(8,128)S(1)}, bf16[64,128]{1,0:T(8,128)(2,1)S(1)}, /*index=5*/f32[2,32,128]{2,1,0:T(8,128)S(1)}, ...), branch_computations={%region_0.1_spmd, %region_1.2_spmd} | conditional | bytes 8 | solution.py:709
  162.7 7.7 %turn.3 = (f32[128,64,128]{2,1,0:T(8,128)}, f32[128,64,128]{2,1,0:T(8,128)}) custom-call(f32[128,64,128]{2,1,0:T(8,128)} %bitcast.19, f32[128,64,128]{2,1,0:T(8,128)S(1)} %get-tuple-element.42.kept_ref), custom_call_target="tpu_custom_call" | custom-call | tf_op jit(solution)/shard_map/cond/branch_1_fun/turn/pallas_call | solution.py:636
  (3 shorter events, 0.0 us)
Async XLA Ops:
  0.6 7.7 %copy-start.1 = (f32[512,512]{1,0:T(8,128)S(1)}, f32[512,512]{1,0:T(8,128)}, u32[]{:S(2)}) copy-start(f32[512,512]{1,0:T(8,128)} %constant.19.clone) | copy-start | bytes 3145732
  6.7 5.5 %copy-start.2 = (f32[2,32]{1,0:T(2,128)S(1)}, f32[2,32]{1,0:T(2,128)}, u32[]{:S(2)}) copy-start(f32[2,32]{1,0:T(2,128)} %constant.18.clone) | copy-start | bytes 772
  6.7 5.5 %copy-start = (f32[128,64,128]{2,1,0:T(8,128)S(1)}, f32[128,64,128]{2,1,0:T(8,128)}, u32[]{:S(2)}) copy-start(f32[128,64,128]{2,1,0:T(8,128)} %log_crit.1) | copy-start | bytes 12582916
